TPU v7x, 32 devices: a whole 2x2x4 slice. The times are simulated.
32 devices in a mesh: tok: 4 (over z), hid: 8 (over y, x, core).
Axes of the slice: x: 2, y: 2, z: 4, core: 2. Of those that a mesh axis runs over, the one named last changes fastest.
Arguments:
- activations: bfloat16 [512, 4096], P('tok'), may hold values from -12 to 12
- cotangent: bfloat16 [512, 8192], P('tok', 'hid'), may hold values from -0.015625 to 0.015625
- left_gram: float32 [32, 1024, 1024], P('hid', 'tok'), may hold values from -0.28125 to 30, as said below
- right_gram: float32 [32, 1024, 1024], P('hid', 'tok'), may hold values from -0.28125 to 30, as said below
- left_root: float32 [32, 1024, 1024], P('hid', 'tok'), may hold values from -0.0115625 to 1.21, as said below
- right_root: float32 [32, 1024, 1024], P('hid', 'tok'), may hold values from -0.0115625 to 1.21, as said below
Outputs:
- left_next: float32 [32, 1024, 1024], P('hid', 'tok')
- right_next: float32 [32, 1024, 1024], P('hid', 'tok')
- left_refined: float32 [32, 1024, 1024], P('hid', 'tok')
- right_refined: float32 [32, 1024, 1024], P('hid', 'tok')
- update: float32 [4, 1024, 8192], P(None, 'tok', 'hid')
Inputs may be any that keep to these rules, and one draw needn't show every extreme that they name: `left_gram`: every block is symmetric and positive definite. `right_gram`: every block is symmetric and positive definite. `left_root`: every block is symmetric. `right_root`: every block is symmetric.
All inputs are finite; a program needn't handle non-finite values.
Results may differ from a plain program's by a relative error of at most 0.019.
Values may be sent and summed in bfloat16 or wider, within the bound.
A program may use at most 128 MiB of HBM per device.

v0:
```python
import functools

import jax
import jax.numpy as jnp
from jax import lax
from jax.experimental import pallas as pl
from jax.experimental.pallas import tpu as pltpu
from jax.sharding import PartitionSpec as P


BETA = 0.95
EPS = 1e-06


def as_sent(value):

    def short(part):
        return part.astype(jnp.bfloat16) if part.dtype == jnp.float32 else part

    return jax.tree.map(short, value)


def partner(block, axis, bit):
    count = lax.axis_size(axis)
    route = []
    for low in range(count):
        high = low | 1 << bit
        if high != low and high < count:
            route += [(low, high), (high, low)]
    return lax.ppermute(block, axis, route)


def newton_rows(gram_rows, root_full, root_rows):
    product = gram_rows.astype(jnp.bfloat16)
    for _ in range(4):
        product = jnp.einsum(
            "brk,bkc->brc", product, root_full, preferred_element_type=jnp.float32
        ).astype(jnp.bfloat16)
    final = jnp.einsum("brk,bkc->brc", product, root_full, preferred_element_type=jnp.float32)
    return (5.0 * root_rows - final) / 4.0


def butterfly(pieces, swapper):
    group_size = pieces.shape[0]
    position = lax.axis_index("hid") % group_size
    ordering = jnp.bitwise_xor(jnp.arange(group_size, dtype=jnp.int32), position)
    holding = jnp.take(pieces, ordering, axis=0)
    for bit_level in range(group_size.bit_length() - 1):
        stride = 1 << bit_level
        shaped = holding.reshape((group_size // (2 * stride), 2, stride) + holding.shape[1:])
        incoming = swapper(shaped[:, 1], bit_level)
        holding = jnp.stack([shaped[:, 0], incoming], axis=1).reshape(holding.shape)
    return jnp.take(holding, ordering, axis=0)


def swap_blocks(portion, bit_level):
    return jax.tree.map(
        lambda part, own: part.astype(own.dtype),
        partner(as_sent(portion), "hid", bit_level),
        portion,
    )


def swap_updates(portion, bit_level):
    return jax.tree.map(
        lambda part, own: part.astype(own.dtype),
        partner(as_sent(portion), "hid", bit_level),
        portion,
    )


def make_folder(own_rows, root_low_rows, first_row):
    slab_rows = own_rows.shape[1]

    def absorb(running, portion, offset):
        column_slab = lax.dynamic_slice_in_dim(portion, first_row, slab_rows, 2)
        products = jnp.einsum("brk,bnk->brn", own_rows, portion, preferred_element_type=jnp.float32)
        right_rows = jnp.einsum(
            "bnr,bnk->brk", column_slab, portion, preferred_element_type=jnp.float32
        )
        left_applied = jnp.einsum(
            "brn,bnk->brk", root_low_rows, portion, preferred_element_type=jnp.float32
        )
        return (products, right_rows, left_applied)

    return absorb


def on_device(activations, cotangent, left_gram, right_gram, left_root, right_root):
    owned_blocks, slab_rows, block_size = left_gram.shape
    slab_width = cotangent.shape[1]
    group_size = block_size // slab_width
    block_rows = activations.shape[1] // block_size
    partial_value = jnp.einsum(
        "td,tc->dc", activations, cotangent, preferred_element_type=jnp.float32
    )
    partial_value = partial_value.reshape(block_rows, block_size, slab_width)
    first_row = lax.axis_index("tok") * slab_rows
    left_low = left_root.astype(jnp.bfloat16)
    right_low = right_root.astype(jnp.bfloat16)
    left_full, right_full = (
        lax.all_gather(left_low, "tok", axis=1, tiled=True),
        lax.all_gather(right_low, "tok", axis=1, tiled=True),
    )
    empty = jnp.zeros((owned_blocks, slab_rows, block_size), jnp.float32)
    initial = (empty, empty, empty)
    summed = lax.psum(partial_value.astype(jnp.bfloat16), "tok")
    pieces = summed.reshape(group_size, owned_blocks, block_size, slab_width)
    arrived = butterfly(pieces, swap_blocks)
    full_block = arrived.transpose(1, 2, 0, 3).reshape(owned_blocks, block_size, block_size)
    own_rows = lax.dynamic_slice_in_dim(full_block, first_row, slab_rows, 1)
    folder = make_folder(own_rows, left_low, first_row)
    left_cols, right_rows, left_applied = folder(initial, full_block, 0)
    left_next = BETA * left_gram + left_cols
    right_next = BETA * right_gram + right_rows
    left_refined = newton_rows(left_next, left_full, left_root)
    right_refined = newton_rows(right_next, right_full, right_root)
    precond = jnp.einsum(
        "brk,bkc->brc",
        left_applied.astype(jnp.bfloat16),
        right_full,
        preferred_element_type=jnp.float32,
    )
    squares = lax.psum(jnp.sum(precond * precond, axis=(1, 2)), "tok")
    scale = jnp.sqrt(squares / (block_size * block_size) + EPS)
    scaled = precond / scale[:, None, None]
    outgoing = scaled.reshape(owned_blocks, slab_rows, group_size, slab_width).transpose(2, 0, 1, 3)
    returned = butterfly(outgoing, swap_updates)
    update = returned.reshape(block_rows, slab_rows, slab_width)
    return (left_next, right_next, left_refined, right_refined, update)


RIGHT_PARTS = (4,)
LEFT_PARTS = (2, 2)
VMEM = 60 * 1024 * 1024


def part_ranges(sizes, blocks):
    if sum(sizes) != blocks:
        sizes = (blocks,)
    ranges, first = [], 0
    for size in sizes:
        ranges.append((first, size))
        first += size
    return ranges


def pair_swap(value, axis, mask):
    count = lax.axis_size(axis)
    return lax.ppermute(value, axis, [(i, i ^ mask) for i in range(count)])


def strip_rows(blocks):
    return -(-blocks // 16) * 16


def diagonal_masks(half):
    row = lax.broadcasted_iota(jnp.int32, (half, half), 0)
    column = lax.broadcasted_iota(jnp.int32, (half, half), 1)
    return row, column


def pack_body(ranges, root_ref, fold_ref, *outs):
    total = ranges[-1][0] + ranges[-1][1]
    tile = root_ref.shape[1]
    half = tile // 2
    b = pl.program_id(0)
    me = lax.axis_index("tok")
    low = me < 2

    def tile_at(index):
        return root_ref[0, :, pl.ds(pl.multiple_of(index * tile, tile), tile)]

    own = tile_at(me)
    first, last = own[:half, :half], own[half:, half:]
    row, column = diagonal_masks(half)
    folded = jnp.where(row <= column, first, last)
    place = pl.ds(pl.multiple_of(b * half, half), half)
    fold_ref[place, :half] = folded.astype(jnp.bfloat16)
    fold_ref[place, half:] = own[:half, half:].astype(jnp.bfloat16)
    diagonal = jnp.sum(jnp.where(row == column, last, 0.0), axis=0, keepdims=True)
    strip = strip_rows(total)
    strip_at = pl.ds(total * half, strip)
    line = lax.broadcasted_iota(jnp.int32, (strip, half), 0)

    @pl.when(b == 0)
    def _():
        fold_ref[strip_at, :] = jnp.zeros((strip, tile), jnp.bfloat16)

    held = fold_ref[strip_at, :half].astype(jnp.float32)
    fold_ref[strip_at, :half] = jnp.where(line == b, diagonal, held).astype(jnp.bfloat16)
    near = jnp.where(low, 2, 1)
    far = jnp.where(low, 3, 0)
    mate = jnp.where(me % 2 == 0, me + 1, me - 1)
    for at, (start, size) in enumerate(ranges):
        wide, thin = outs[2 * at], outs[2 * at + 1]

        @pl.when((b >= start) & (b < start + size))
        def _():
            slot = b - start
            wide[pl.ds(pl.multiple_of(slot * 2 * tile, tile), tile), :] = tile_at(near).astype(jnp.bfloat16)
            wide[pl.ds(pl.multiple_of(slot * 2 * tile + tile, tile), tile), :] = tile_at(far).astype(jnp.bfloat16)
            thin[pl.ds(pl.multiple_of(slot * tile, tile), tile), :] = tile_at(mate).astype(jnp.bfloat16)


def pack(roots, ranges):
    blocks, tile, order = roots.shape
    shapes = [jax.ShapeDtypeStruct((blocks * (tile // 2) + strip_rows(blocks), tile), jnp.bfloat16)]
    for _, size in ranges:
        shapes.append(jax.ShapeDtypeStruct((size * 2 * tile, tile), jnp.bfloat16))
        shapes.append(jax.ShapeDtypeStruct((size * tile, tile), jnp.bfloat16))
    return pl.pallas_call(
        functools.partial(pack_body, ranges),
        grid=(blocks,),
        in_specs=[pl.BlockSpec((1, tile, order), lambda b: (b, 0, 0))],
        out_specs=[pl.BlockSpec(one.shape, lambda b: (0, 0)) for one in shapes],
        out_shape=shapes,
        cost_estimate=pl.CostEstimate(
            flops=2 * blocks * tile * order, bytes_accessed=6 * blocks * tile * order, transcendentals=0
        ),
        compiler_params=pltpu.CompilerParams(vmem_limit_bytes=VMEM),
    )(roots)


def exchange(roots, ranges):
    fold, *rest = pack(roots, ranges)
    folds = []
    for mask in (1, 2, 3):
        folds.append(pair_swap(fold, "tok", mask))
    parts = []
    for at in range(len(ranges)):
        wide, thin = rest[2 * at], rest[2 * at + 1]
        wide = pair_swap(wide, "tok", 1)
        skip = lax.ppermute(thin, "tok", [(2, 0), (1, 3)])
        following = lax.ppermute(thin, "tok", [(2, 1), (1, 2)])
        parts.append((wide, skip, following))
    return folds, parts


def front_body(place_ref, act, cot, left_gram, right_gram, left_root, pieces, left_next, right_next, applied, tokens, grad):
    b = pl.program_id(0)
    rows, order = left_gram.shape[1:]
    group, width = act.shape[0], pieces[0].shape[1]
    hid, first_row = place_ref[0], place_ref[1] * rows

    @pl.when(b == 0)
    def _():
        tokens[:group, :] = act[...]
        for mask, piece in enumerate(pieces):
            column = jnp.bitwise_xor(hid, mask) * width
            tokens[group:, pl.ds(pl.multiple_of(column, width), width)] = piece[...]

    both = (((0,), (0,)), ((), ()))

    @pl.loop(0, order // rows)
    def _(step):
        column = pl.multiple_of(b * order + step * rows, rows)
        grad[pl.ds(pl.multiple_of(step * rows, rows), rows), :] = lax.dot_general(
            tokens[:, pl.ds(column, rows)], cot[...], both, preferred_element_type=jnp.float32
        ).astype(jnp.bfloat16)

    slab = pl.ds(pl.multiple_of(first_row, rows), rows)
    product = lax.dot_general(
        grad[slab, :], grad[...], (((1,), (1,)), ((), ())), preferred_element_type=jnp.float32
    )
    left_next[0] = BETA * left_gram[0] + product
    product = lax.dot_general(grad[:, slab], grad[...], both, preferred_element_type=jnp.float32)
    right_next[0] = BETA * right_gram[0] + product
    applied[0] = jnp.dot(
        left_root[0].astype(jnp.bfloat16), grad[...], preferred_element_type=jnp.float32
    ).astype(jnp.bfloat16)


def front(place, act, cot, pieces, left_gram, right_gram, left_root):
    blocks, rows, order = left_gram.shape
    count = len(pieces)
    depth = cot.shape[0]

    def body(place_ref, act_ref, cot_ref, lg, rg, lr, *refs):
        front_body(place_ref, act_ref, cot_ref, lg, rg, lr, refs[:count], *refs[count:])

    def whole(array):
        return pl.BlockSpec(array.shape, lambda b, s: (0,) * array.ndim)

    slab = pl.BlockSpec((1, rows, order), lambda b, s: (b, 0, 0))
    shape = (blocks, rows, order)
    return pl.pallas_call(
        body,
        grid_spec=pltpu.PrefetchScalarGridSpec(
            num_scalar_prefetch=1,
            grid=(blocks,),
            in_specs=[whole(act), whole(cot), slab, slab, slab] + [whole(one) for one in pieces],
            out_specs=[slab, slab, slab],
            scratch_shapes=[
                pltpu.VMEM((depth, act.shape[1]), jnp.bfloat16),
                pltpu.VMEM((order, order), jnp.bfloat16),
            ],
        ),
        out_shape=[
            jax.ShapeDtypeStruct(shape, jnp.float32),
            jax.ShapeDtypeStruct(shape, jnp.float32),
            jax.ShapeDtypeStruct(shape, jnp.bfloat16),
        ],
        cost_estimate=pl.CostEstimate(
            flops=2 * blocks * order * order * (depth + 3 * rows),
            bytes_accessed=blocks * rows * order * 22,
            transcendentals=0,
        ),
        compiler_params=pltpu.CompilerParams(vmem_limit_bytes=VMEM),
    )(place, act, cot, left_gram, right_gram, left_root, *pieces)


def chain_body(first, total, with_update, with_base, *refs):
    next_ref, root_ref, fold1, fold2, fold3, wide, skip, following = refs[:8]
    refs = refs[8:]
    if with_update:
        applied, refs = refs[0], refs[1:]
    if with_base:
        refs = refs[1:]
    refined, refs = refs[0], refs[1:]
    if with_update:
        precond, refs = refs[0], refs[1:]
    full, product = refs
    tile = root_ref.shape[1]
    half = tile // 2
    slot = pl.program_id(0)
    b = slot + first
    me = lax.axis_index("tok")
    low = me < 2
    end = (me == 0) | (me == 3)
    near = jnp.where(low, 2, 1)
    far = jnp.where(low, 3, 0)
    mate = jnp.where(me % 2 == 0, me + 1, me - 1)

    def at(index, extra=0, size=tile):
        return pl.ds(pl.multiple_of(index * tile + extra, half), size)

    def flipped(value):
        return value.astype(jnp.float32).T.astype(jnp.bfloat16)

    full[at(me), :] = root_ref[0].astype(jnp.bfloat16)
    for other in (mate, near, far):
        full[at(other), at(me)] = root_ref[0, :, at(other)].T.astype(jnp.bfloat16)
    row, column = diagonal_masks(half)
    strip = strip_rows(total)
    line = lax.broadcasted_iota(jnp.int32, (strip, half), 0)
    place = pl.ds(pl.multiple_of(b * half, half), half)

    def unfold(index, fold):
        folded = fold[place, :half].astype(jnp.float32)
        corner = fold[place, half:]
        turned = folded.T
        strips = fold[pl.ds(total * half, strip), :half].astype(jnp.float32)
        diagonal = jnp.sum(jnp.where(line == b, strips, 0.0), axis=0, keepdims=True)
        full[at(index, 0, half), at(index, 0, half)] = jnp.where(row <= column, folded, turned).astype(jnp.bfloat16)
        lower = jnp.where(row == column, diagonal, jnp.where(row > column, folded, turned))
        full[at(index, half, half), at(index, half, half)] = lower.astype(jnp.bfloat16)
        full[at(index, 0, half), at(index, half, half)] = corner
        full[at(index, half, half), at(index, 0, half)] = flipped(corner)

    def both(i, j, value):
        full[at(i), at(j)] = value
        full[at(j), at(i)] = flipped(value)

    unfold(mate, fold1)
    unfold(jnp.where(low, me + 2, me - 2), fold2)
    unfold(3 - me, fold3)
    both(mate, near, wide[pl.ds(pl.multiple_of(slot * 2 * tile, tile), tile), :])
    both(mate, far, wide[pl.ds(pl.multiple_of(slot * 2 * tile + tile, tile), tile), :])
    thin = pl.ds(pl.multiple_of(slot * tile, tile), tile)
    both(near, far, jnp.where(end, skip[thin, :], following[thin, :]))
    if with_update:
        precond[0] = jnp.dot(applied[0], full[...], preferred_element_type=jnp.float32)
    product[...] = next_ref[0].astype(jnp.bfloat16)

    @pl.loop(0, 4)
    def _(repeat):
        product[...] = jnp.dot(
            product[...], full[...], preferred_element_type=jnp.float32
        ).astype(jnp.bfloat16)

    final = jnp.dot(product[...], full[...], preferred_element_type=jnp.float32)
    refined[0] = (5.0 * root_ref[0] - final) / 4.0


def chain(next_rows, roots, folds, tiles, applied, base, first, size):
    blocks, rows, order = roots.shape

    def slab(array):
        return pl.BlockSpec((1,) + array.shape[1:], lambda b: (b + first, 0, 0))

    def whole(array):
        return pl.BlockSpec(array.shape, lambda b: (0, 0))

    operands = [next_rows, roots, *folds, *tiles]
    specs = [slab(next_rows), slab(roots)] + [whole(one) for one in (*folds, *tiles)]
    if applied is not None:
        operands.append(applied)
        specs.append(slab(applied))
    aliases = {}
    if base is not None:
        aliases = {len(operands): 0}
        operands.append(base)
        specs.append(pl.BlockSpec(memory_space=pl.ANY))
    out = jax.ShapeDtypeStruct((blocks, rows, order), jnp.float32)
    outputs = [out] if applied is None else [out, out]
    matmuls = 5 if applied is None else 6
    return pl.pallas_call(
        functools.partial(chain_body, first, blocks, applied is not None, base is not None),
        grid=(size,),
        in_specs=specs,
        out_specs=[slab(one) for one in outputs],
        out_shape=outputs,
        input_output_aliases=aliases,
        scratch_shapes=[
            pltpu.VMEM((order, order), jnp.bfloat16),
            pltpu.VMEM((rows, order), jnp.bfloat16),
        ],
        cost_estimate=pl.CostEstimate(
            flops=2 * matmuls * size * rows * order * order,
            bytes_accessed=size * rows * order * 20,
            transcendentals=0,
        ),
        compiler_params=pltpu.CompilerParams(vmem_limit_bytes=VMEM),
    )(*operands)


def gather_tokens(activations, cotangent):
    count = lax.axis_size("hid")
    place = lax.axis_index("hid")
    width = activations.shape[1] // count
    piece = lax.dynamic_slice_in_dim(activations, place * width, width, 1)
    arrived, cots = [], [cotangent]
    for mask in (1, 2, 3):
        arrived.append(pair_swap(piece, "tok", mask))
    for mask in (1, 2, 3):
        cots.append(pair_swap(cotangent, "tok", mask))
    mine = jnp.concatenate(arrived, axis=0)
    held = [mine]
    for mask in range(2, count, 2):
        held.append(pair_swap(mine, "hid", mask))
    pieces = []
    for one in held:
        pieces += [one, pair_swap(one, "hid", 1)]
    return pieces, jnp.concatenate(cots, axis=0)


def line_program(activations, cotangent, left_gram, right_gram, left_root, right_root):
    blocks, _, order = left_gram.shape
    right_ranges = part_ranges(RIGHT_PARTS, blocks)
    left_ranges = part_ranges(LEFT_PARTS, blocks)
    pieces, cots = gather_tokens(activations, cotangent)
    right_folds, right_tiles = exchange(right_root, right_ranges)
    left_folds, left_tiles = exchange(left_root, left_ranges)
    place = jnp.stack([lax.axis_index("hid"), lax.axis_index("tok")]).astype(jnp.int32)
    left_next, right_next, applied = front(
        place, activations, cots, pieces, left_gram, right_gram, left_root
    )
    (first, size), = right_ranges
    right_refined, precond = chain(
        right_next, right_root, right_folds, right_tiles[0], applied, None, first, size
    )
    local = jnp.sum(precond * precond, axis=(1, 2))
    squares = local
    for mask in (1, 2, 3):
        squares = squares + pair_swap(local, "tok", mask)
    scale = jnp.sqrt(squares / (order * order) + EPS)
    update = precond / scale[:, None, None]
    left_refined = None
    for at, (first, size) in enumerate(left_ranges):
        (left_refined,) = chain(
            left_next, left_root, left_folds, left_tiles[at], None, left_refined, first, size
        )
    return left_next, right_next, left_refined, right_refined, update


def solution(mesh):
    in_specs = (
        P("tok", None),
        P("tok", "hid"),
        P("hid", "tok", None),
        P("hid", "tok", None),
        P("hid", "tok", None),
        P("hid", "tok", None),
    )
    out_specs = (
        P("hid", "tok", None),
        P("hid", "tok", None),
        P("hid", "tok", None),
        P("hid", "tok", None),
        P(None, "tok", "hid"),
    )

    def run(*operands):
        activations, cotangent, left_gram = (one.shape for one in operands[:3])
        tok, hid = mesh.shape["tok"], mesh.shape["hid"]
        whole_blocks = cotangent[1] == left_gram[2]
        one_column = left_gram[0] == activations[1] // left_gram[2]
        even = hid >= 2 and hid & (hid - 1) == 0
        if tok == 4 and whole_blocks and one_column and even:
            return line_program(*operands)
        return on_device(*operands)

    return jax.shard_map(
        run, mesh=mesh, in_specs=in_specs, out_specs=out_specs, check_vma=False
    )
```

profile of v0, /device:TPU:0, one launch (start us, length us, event | category | flops | bytes accessed | tf_op | source)
XLA Modules:
  0.0 198.7 jit_solution(17279349283556564479)
XLA Ops:
  0.6 0.0 copy-start.1
  0.6 1.0 constant_dynamic-slice_fusion
  1.6 3.1 %collective-permute-start.3 = (bf16[128,512]{1,0:T(8,128)(2,1)S(1)}, bf16[128,512]{1,0:T(8,128)(2,1)S(1)}, u32[]{:S(2)}, u32[]{:S(2)}) collective-permute-start(bf16[128,512]{1,0:T(8,128)(2,1)S(1)} %constant_dynamic-slice_fusion), channel_id=1, source_target_pairs={{0,8},{8,0},{16,24},{24,16},{1,9},{9,1},{17,25},{25,17},{2,10},{10... | collective-permute-start | bytes 393224 | tf_op jit(solution)/shard_map/ppermute | solution.py:150
  4.7 2.6 %collective-permute-start.4 = (bf16[128,512]{1,0:T(8,128)(2,1)S(1)}, bf16[128,512]{1,0:T(8,128)(2,1)S(1)}, u32[]{:S(2)}, u32[]{:S(2)}) collective-permute-start(bf16[128,512]{1,0:T(8,128)(2,1)S(1)} %constant_dynamic-slice_fusion), channel_id=1, source_target_pairs={{0,16},{8,24},{16,0},{24,8},{1,17},{9,25},{17,1},{25,9},{2,18},{10... | collective-permute-start | bytes 393224 | tf_op jit(solution)/shard_map/ppermute | solution.py:150
  7.3 0.0 collective-permute-start.5
  7.3 1.9 collective-permute-start.1
  9.2 2.5 %collective-permute-start = (bf16[128,1024]{1,0:T(8,128)(2,1)}, bf16[128,1024]{1,0:T(8,128)(2,1)S(1)}, u32[]{:S(2)}, u32[]{:S(2)}) collective-permute-start(bf16[128,1024]{1,0:T(8,128)(2,1)} %param.7), channel_id=1, source_target_pairs={{0,8},{8,0},{16,24},{24,16},{1,9},{9,1},{17,25},{25,17},{2,10},{10... | collective-permute-start | bytes 786440 | tf_op jit(solution)/shard_map/ppermute | solution.py:150
  11.7 4.3 %shard_map.102 = (bf16[528,256]{1,0:T(8,128)(2,1)}, bf16[1024,256]{1,0:T(8,128)(2,1)}, bf16[512,256]{1,0:T(8,128)(2,1)}, bf16[1024,256]{1,0:T(8,128)(2,1)}, bf16[512,256]{1,0:T(8,128)(2,1)}) custom-call(f32[4,256,1024]{2,1,0:T(8,128)} %refs_1_.4), custom_call_target="tpu_custom_call" | custom-call | flops 2097152 | bytes 6291456 | tf_op jit(solution)/shard_map/pallas_call | solution.py:212
  16.0 0.1 collective-permute-start.2
  16.1 7.2 %collective-permute-done.4 = bf16[128,512]{1,0:T(8,128)(2,1)S(1)} collective-permute-done((bf16[128,512]{1,0:T(8,128)(2,1)S(1)}, bf16[128,512]{1,0:T(8,128)(2,1)S(1)}, u32[]{:S(2)}, u32[]{:S(2)}) %collective-permute-start.4) | collective-permute-done | bytes 131104 | tf_op jit(solution)/shard_map/ppermute | solution.py:150
  23.2 0.7 collective-permute-start.18
  23.9 0.0 collective-permute-done.5
  23.9 1.3 collective-permute-start.17
  25.3 12.0 %collective-permute-done.1 = bf16[128,1024]{1,0:T(8,128)(2,1)S(1)} collective-permute-done((bf16[128,1024]{1,0:T(8,128)(2,1)}, bf16[128,1024]{1,0:T(8,128)(2,1)S(1)}, u32[]{:S(2)}, u32[]{:S(2)}) %collective-permute-start.1) | collective-permute-done | bytes 262176 | tf_op jit(solution)/shard_map/ppermute | solution.py:150
  37.3 2.4 %collective-permute-start.11 = (bf16[384,512]{1,0:T(8,128)(2,1)S(1)}, bf16[384,512]{1,0:T(8,128)(2,1)S(1)}, u32[]{:S(2)}, u32[]{:S(2)}) collective-permute-start(bf16[384,512]{1,0:T(8,128)(2,1)S(1)} %constant_dynamic-update-slice_fusion.refs_0_), channel_id=1, source_target_pairs={{0,6},{1,7},{2,4},{3,5},{4,2},{5,3},{6,0},{7,1},{8,14},{9,15},{10,... | collective-permute-start | bytes 1179656 | tf_op jit(solution)/shard_map/ppermute | solution.py:150
  39.7 0.0 collective-permute-done
  39.7 0.5 collective-permute-start.9
  40.2 0.5 collective-permute-start.7
  40.8 0.7 collective-permute-start.21
  41.5 12.7 %collective-permute-done.17.refs_6_ = bf16[512,256]{1,0:T(8,128)(2,1)S(1)} collective-permute-done((bf16[512,256]{1,0:T(8,128)(2,1)}, bf16[512,256]{1,0:T(8,128)(2,1)S(1)}, u32[]{:S(2)}, u32[]{:S(2)}) %collective-permute-start.17) | collective-permute-done | bytes 262176 | tf_op jit(solution)/shard_map/ppermute | solution.py:234
  54.1 1.3 collective-permute-start.20
  55.4 0.0 collective-permute-done.21.refs_7_
  55.5 0.1 collective-permute-start.6
  55.5 0.0 collective-permute-done.11.refs_6_
  55.6 0.5 collective-permute-start.12
  56.0 0.0 collective-permute-done.9.refs_4_
  56.0 0.1 collective-permute-start.10
  56.1 0.0 collective-permute-done.7.refs_2_
  56.1 0.0 copy-done.16
  56.2 0.4 collective-permute-start.8
  56.6 7.5 %collective-permute-done.20.refs_6_ = bf16[512,256]{1,0:T(8,128)(2,1)} collective-permute-done((bf16[512,256]{1,0:T(8,128)(2,1)}, bf16[512,256]{1,0:T(8,128)(2,1)}, u32[]{:S(2)}, u32[]{:S(2)}) %collective-permute-start.20) | collective-permute-done | bytes 262176 | tf_op jit(solution)/shard_map/ppermute | solution.py:234
  64.1 3.0 %collective-permute-start.15 = (bf16[528,256]{1,0:T(8,128)(2,1)}, bf16[528,256]{1,0:T(8,128)(2,1)}, u32[]{:S(2)}, u32[]{:S(2)}) collective-permute-start(bf16[528,256]{1,0:T(8,128)(2,1)} %get-tuple-element.20), channel_id=1, source_target_pairs={{0,24},{8,16},{16,8},{24,0},{1,25},{9,17},{17,9},{25,1},{2,26},{10... | collective-permute-start | bytes 811016 | tf_op jit(solution)/shard_map/ppermute | solution.py:150
  67.1 4.3 %shard_map.105 = (bf16[528,256]{1,0:T(8,128)(2,1)}, bf16[2048,256]{1,0:T(8,128)(2,1)}, bf16[1024,256]{1,0:T(8,128)(2,1)}) custom-call(f32[4,256,1024]{2,1,0:T(8,128)} %refs_1_.5), custom_call_target="tpu_custom_call" | custom-call | flops 2097152 | bytes 6291456 | tf_op jit(solution)/shard_map/pallas_call | solution.py:212
  71.4 0.7 pad_add_fusion.place_ref
  72.0 1.0 pad_maximum_fusion.cot_ref
  73.1 0.0 collective-permute-done.15.refs_4_
  73.1 5.0 %collective-permute-start.14 = (bf16[528,256]{1,0:T(8,128)(2,1)}, bf16[528,256]{1,0:T(8,128)(2,1)}, u32[]{:S(2)}, u32[]{:S(2)}) collective-permute-start(bf16[528,256]{1,0:T(8,128)(2,1)} %get-tuple-element.20), channel_id=1, source_target_pairs={{0,16},{8,24},{16,0},{24,8},{1,17},{9,25},{17,1},{25,9},{2,18},{10... | collective-permute-start | bytes 811016 | tf_op jit(solution)/shard_map/ppermute | solution.py:150
  78.1 0.0 collective-permute-start.13
  78.1 0.0 collective-permute-done.12.refs_7_
  78.1 0.7 copy-done.10
  78.9 1.3 collective-permute-start.16
  80.2 0.7 collective-permute-start.19
  80.9 1.3 collective-permute-start.25
  82.3 20.8 %shard_map.101 = (f32[4,256,1024]{2,1,0:T(8,128)}, f32[4,256,1024]{2,1,0:T(8,128)}, bf16[4,256,1024]{2,1,0:T(8,128)(2,1)}) custom-call(s32[2]{0:T(128)} %pad_add_fusion.place_ref, bf16[128,4096]{1,0:T(8,128)(2,1)} %act_ref.1, bf16[512,1024]{1,0:T(8,128)(2,1)} %pad_maximum_fusion.cot_ref, f32[4,256,1024]{2,1,0:T(8,128)} %lg.1, f32[4,256,1024]{2,1,0:T(8,128)} %rg.1, ...), custom_call_target="tpu_custom_call" | custom-call | flops 10737418240 | bytes 23068672 | tf_op jit(solution)/shard_map/pallas_call | solution.py:287
  103.1 0.7 collective-permute-start.27
  103.8 1.3 collective-permute-start.26
  105.1 13.0 %collective-permute-done.19.refs_5_ = bf16[1024,256]{1,0:T(8,128)(2,1)} collective-permute-done((bf16[1024,256]{1,0:T(8,128)(2,1)S(1)}, bf16[1024,256]{1,0:T(8,128)(2,1)}, u32[]{:S(2)}, u32[]{:S(2)}) %collective-permute-start.19) | collective-permute-done | bytes 524320 | tf_op jit(solution)/shard_map/ppermute | solution.py:150
  118.1 11.3 %shard_map.103.refs_8_ = f32[4,256,1024]{2,1,0:T(8,128)} custom-call(f32[4,256,1024]{2,1,0:T(8,128)} %get-tuple-element.13.refs_0_, f32[4,256,1024]{2,1,0:T(8,128)} %refs_1_.4, bf16[528,256]{1,0:T(8,128)(2,1)} %collective-permute-done.13.refs_2_, bf16[528,256]{1,0:T(8,128)(2,1)} %collective-permute-done.14.refs_3_, ...), custom_call_target="tpu_custom_call" | custom-call | flops 5368709120 | bytes 10485760 | tf_op jit(solution)/shard_map/pallas_call | solution.py:408
  129.4 11.0 %collective-permute-done.24.refs_4_ = bf16[528,256]{1,0:T(8,128)(2,1)S(1)} collective-permute-done((bf16[528,256]{1,0:T(8,128)(2,1)}, bf16[528,256]{1,0:T(8,128)(2,1)S(1)}, u32[]{:S(2)}, u32[]{:S(2)}) %collective-permute-start.24) | collective-permute-done | bytes 270368 | tf_op jit(solution)/shard_map/ppermute | solution.py:150
  140.4 0.0 copy-start.7
  140.4 4.8 %collective-permute-start.22 = (bf16[528,256]{1,0:T(8,128)(2,1)S(1)}, bf16[528,256]{1,0:T(8,128)(2,1)S(1)}, u32[]{:S(2)}, u32[]{:S(2)}) collective-permute-start(bf16[528,256]{1,0:T(8,128)(2,1)S(1)} %copy-done.11), channel_id=1, source_target_pairs={{0,8},{8,0},{16,24},{24,16},{1,9},{9,1},{17,25},{25,17},{2,10},{10... | collective-permute-start | bytes 811016 | tf_op jit(solution)/shard_map/ppermute | solution.py:150
  145.2 11.3 %shard_map.104 = f32[4,256,1024]{2,1,0:T(8,128)} custom-call(f32[4,256,1024]{2,1,0:T(8,128)} %get-tuple-element.13.refs_0_, f32[4,256,1024]{2,1,0:T(8,128)} %refs_1_.4, bf16[528,256]{1,0:T(8,128)(2,1)} %collective-permute-done.13.refs_2_, bf16[528,256]{1,0:T(8,128)(2,1)} %collective-permute-done.14.refs_3_, ...), custom_call_target="tpu_custom_call", output_to_operand_aliasing={{}: (8, {})} | custom-call | flops 5368709120 | bytes 10485760 | tf_op jit(solution)/shard_map/pallas_call | solution.py:408
  156.5 6.2 %collective-permute-done.22.refs_2_ = bf16[528,256]{1,0:T(8,128)(2,1)S(1)} collective-permute-done((bf16[528,256]{1,0:T(8,128)(2,1)S(1)}, bf16[528,256]{1,0:T(8,128)(2,1)S(1)}, u32[]{:S(2)}, u32[]{:S(2)}) %collective-permute-start.22) | collective-permute-done | bytes 270368 | tf_op jit(solution)/shard_map/ppermute | solution.py:150
  162.7 0.7 copy-done.13
  163.4 0.2 copy-done.8
  163.6 0.3 copy-done.3
  163.9 23.5 %shard_map.106 = (f32[4,256,1024]{2,1,0:T(8,128)}, f32[4,256,1024]{2,1,0:T(8,128)}) custom-call(f32[4,256,1024]{2,1,0:T(8,128)} %get-tuple-element.14.refs_0_, f32[4,256,1024]{2,1,0:T(8,128)} %refs_1_.5, bf16[528,256]{1,0:T(8,128)(2,1)} %copy-done.13, bf16[528,256]{1,0:T(8,128)(2,1)} %collective-permute-done.23.refs_3_, bf16[528,256]{1,0:T(8,128)(2,1)} %copy-done.12, ...), custom_call_target="tpu_custom_call" | custom-call | flops 12884901888 | bytes 20971520 | tf_op jit(solution)/shard_map/pallas_call | solution.py:408
  187.4 2.8 %multiply_reduce_fusion = f32[4]{0:T(128)S(1)} fusion(f32[4,256,1024]{2,1,0:T(8,128)} %get-tuple-element.30), kind=kLoop, calls=%fused_computation | loop fusion | flops 2097148 | bytes 4194320 | tf_op jit(solution)/shard_map/reduce_sum | solution.py:463
  190.2 0.5 collective-permute-start.30
  190.7 0.5 collective-permute-start.29
  191.2 3.4 %collective-permute-start.28 = (f32[4]{0:T(128)S(1)}, f32[4]{0:T(128)S(1)}, u32[]{:S(2)}, u32[]{:S(2)}) collective-permute-start(f32[4]{0:T(128)S(1)} %multiply_reduce_fusion), channel_id=1, source_target_pairs={{0,8},{8,0},{16,24},{24,16},{1,9},{9,1},{17,25},{25,17},{2,10},{10... | collective-permute-start | bytes 56 | tf_op jit(solution)/shard_map/ppermute | solution.py:150
  194.6 1.0 collective-permute-done.30
  195.6 0.6 collective-permute-done.28
  196.1 2.6 %broadcast_divide_fusion = f32[4,256,1024]{2,1,0:T(8,128)} fusion(f32[4,256,1024]{2,1,0:T(8,128)S(1)} %copy-done, f32[4]{0:T(128)S(1)} %add_sqrt_fusion), kind=kLoop, calls=%fused_computation.1 | loop fusion | flops 1048576 | bytes 8388624 | tf_op jit(solution)/shard_map/div | solution.py:468
  (47 shorter events, 0.1 us)
Async XLA Ops:
  0.6 15.3 %copy-start.1 = (bf16[128,1024]{1,0:T(8,128)(2,1)S(1)}, bf16[128,1024]{1,0:T(8,128)(2,1)}, u32[]{:S(2)}) copy-start(bf16[128,1024]{1,0:T(8,128)(2,1)} %param.7) | copy-start | bytes 786436
  1.6 14.4 %collective-permute-start.3 = (bf16[128,512]{1,0:T(8,128)(2,1)S(1)}, bf16[128,512]{1,0:T(8,128)(2,1)S(1)}, u32[]{:S(2)}, u32[]{:S(2)}) collective-permute-start(bf16[128,512]{1,0:T(8,128)(2,1)S(1)} %constant_dynamic-slice_fusion), channel_id=1, source_target_pairs={{0,8},{8,0},{16,24},{24,16},{1,9},{9,1},{17,25},{25,17},{2,10},{10... | collective-permute-start | bytes 393224 | tf_op jit(solution)/shard_map/ppermute | solution.py:150
  4.7 18.5 %collective-permute-start.4 = (bf16[128,512]{1,0:T(8,128)(2,1)S(1)}, bf16[128,512]{1,0:T(8,128)(2,1)S(1)}, u32[]{:S(2)}, u32[]{:S(2)}) collective-permute-start(bf16[128,512]{1,0:T(8,128)(2,1)S(1)} %constant_dynamic-slice_fusion), channel_id=1, source_target_pairs={{0,16},{8,24},{16,0},{24,8},{1,17},{9,25},{17,1},{25,9},{2,18},{10... | collective-permute-start | bytes 393224 | tf_op jit(solution)/shard_map/ppermute | solution.py:150
  7.3 16.6 %collective-permute-start.5 = (bf16[128,512]{1,0:T(8,128)(2,1)S(1)}, bf16[128,512]{1,0:T(8,128)(2,1)S(1)}, u32[]{:S(2)}, u32[]{:S(2)}) collective-permute-start(bf16[128,512]{1,0:T(8,128)(2,1)S(1)} %constant_dynamic-slice_fusion), channel_id=1, source_target_pairs={{0,24},{8,16},{16,8},{24,0},{1,25},{9,17},{17,9},{25,1},{2,26},{10... | collective-permute-start | bytes 393224 | tf_op jit(solution)/shard_map/ppermute | solution.py:150
  7.3 30.0 %collective-permute-start.1 = (bf16[128,1024]{1,0:T(8,128)(2,1)}, bf16[128,1024]{1,0:T(8,128)(2,1)S(1)}, u32[]{:S(2)}, u32[]{:S(2)}) collective-permute-start(bf16[128,1024]{1,0:T(8,128)(2,1)} %param.7), channel_id=1, source_target_pairs={{0,16},{8,24},{16,0},{24,8},{1,17},{9,25},{17,1},{25,9},{2,18},{10... | collective-permute-start | bytes 786440 | tf_op jit(solution)/shard_map/ppermute | solution.py:150
  9.2 30.5 %collective-permute-start = (bf16[128,1024]{1,0:T(8,128)(2,1)}, bf16[128,1024]{1,0:T(8,128)(2,1)S(1)}, u32[]{:S(2)}, u32[]{:S(2)}) collective-permute-start(bf16[128,1024]{1,0:T(8,128)(2,1)} %param.7), channel_id=1, source_target_pairs={{0,8},{8,0},{16,24},{24,16},{1,9},{9,1},{17,25},{25,17},{2,10},{10... | collective-permute-start | bytes 786440 | tf_op jit(solution)/shard_map/ppermute | solution.py:150
  16.0 62.9 %copy-start.4 = (bf16[1024,256]{1,0:T(8,128)(2,1)S(1)}, bf16[1024,256]{1,0:T(8,128)(2,1)}, u32[]{:S(2)}) copy-start(bf16[1024,256]{1,0:T(8,128)(2,1)} %get-tuple-element.21) | copy-start | bytes 1572868
  16.0 64.3 %copy-start.5 = (bf16[1024,256]{1,0:T(8,128)(2,1)S(1)}, bf16[1024,256]{1,0:T(8,128)(2,1)}, u32[]{:S(2)}) copy-start(bf16[1024,256]{1,0:T(8,128)(2,1)} %get-tuple-element.23) | copy-start | bytes 1572868
  16.0 24.3 %collective-permute-start.2 = (bf16[128,1024]{1,0:T(8,128)(2,1)S(1)}, bf16[128,1024]{1,0:T(8,128)(2,1)S(1)}, u32[]{:S(2)}, u32[]{:S(2)}) collective-permute-start(bf16[128,1024]{1,0:T(8,128)(2,1)S(1)} %copy-done.1), channel_id=1, source_target_pairs={{0,24},{8,16},{16,8},{24,0},{1,25},{9,17},{17,9},{25,1},{2,26},{10... | collective-permute-start | bytes 786440 | tf_op jit(solution)/shard_map/ppermute | solution.py:150
  23.2 17.5 %collective-permute-start.18 = (bf16[512,256]{1,0:T(8,128)(2,1)}, bf16[512,256]{1,0:T(8,128)(2,1)S(1)}, u32[]{:S(2)}, u32[]{:S(2)}) collective-permute-start(bf16[512,256]{1,0:T(8,128)(2,1)} %get-tuple-element.22), channel_id=1, source_target_pairs={{16,8},{8,16},{17,9},{9,17},{18,10},{10,18},{19,11},{11,19},{20,12... | collective-permute-start | bytes 786440 | tf_op jit(solution)/shard_map/ppermute | solution.py:235
  23.9 30.2 %collective-permute-start.17 = (bf16[512,256]{1,0:T(8,128)(2,1)}, bf16[512,256]{1,0:T(8,128)(2,1)S(1)}, u32[]{:S(2)}, u32[]{:S(2)}) collective-permute-start(bf16[512,256]{1,0:T(8,128)(2,1)} %get-tuple-element.22), channel_id=1, source_target_pairs={{16,0},{8,24},{17,1},{9,25},{18,2},{10,26},{19,3},{11,27},{20,4},{... | collective-permute-start | bytes 786440 | tf_op jit(solution)/shard_map/ppermute | solution.py:234
  25.3 57.0 %copy-start.2 = (bf16[384,512]{1,0:T(8,128)(2,1)}, bf16[384,512]{1,0:T(8,128)(2,1)S(1)}, u32[]{:S(2)}) copy-start(bf16[384,512]{1,0:T(8,128)(2,1)S(1)} %constant_dynamic-update-slice_fusion.refs_0_) | copy-start | bytes 1179652
  37.3 18.3 %collective-permute-start.11 = (bf16[384,512]{1,0:T(8,128)(2,1)S(1)}, bf16[384,512]{1,0:T(8,128)(2,1)S(1)}, u32[]{:S(2)}, u32[]{:S(2)}) collective-permute-start(bf16[384,512]{1,0:T(8,128)(2,1)S(1)} %constant_dynamic-update-slice_fusion.refs_0_), channel_id=1, source_target_pairs={{0,6},{1,7},{2,4},{3,5},{4,2},{5,3},{6,0},{7,1},{8,14},{9,15},{10,... | collective-permute-start | bytes 1179656 | tf_op jit(solution)/shard_map/ppermute | solution.py:150
  39.7 16.3 %collective-permute-start.9 = (bf16[384,512]{1,0:T(8,128)(2,1)S(1)}, bf16[384,512]{1,0:T(8,128)(2,1)}, u32[]{:S(2)}, u32[]{:S(2)}) collective-permute-start(bf16[384,512]{1,0:T(8,128)(2,1)S(1)} %constant_dynamic-update-slice_fusion.refs_0_), channel_id=1, source_target_pairs={{0,4},{1,5},{2,6},{3,7},{4,0},{5,1},{6,2},{7,3},{8,12},{9,13},{10,... | collective-permute-start | bytes 1179656 | tf_op jit(solution)/shard_map/ppermute | solution.py:150
  40.2 15.9 %collective-permute-start.7 = (bf16[384,512]{1,0:T(8,128)(2,1)S(1)}, bf16[384,512]{1,0:T(8,128)(2,1)}, u32[]{:S(2)}, u32[]{:S(2)}) collective-permute-start(bf16[384,512]{1,0:T(8,128)(2,1)S(1)} %constant_dynamic-update-slice_fusion.refs_0_), channel_id=1, source_target_pairs={{0,2},{1,3},{2,0},{3,1},{4,6},{5,7},{6,4},{7,5},{8,10},{9,11},{10,... | collective-permute-start | bytes 1179656 | tf_op jit(solution)/shard_map/ppermute | solution.py:150
  40.8 14.6 %copy-start.14 = (bf16[512,256]{1,0:T(8,128)(2,1)}, bf16[512,256]{1,0:T(8,128)(2,1)S(1)}, u32[]{:S(2)}) copy-start(bf16[512,256]{1,0:T(8,128)(2,1)S(1)} %collective-permute-done.18.refs_7_) | copy-start | bytes 786436
  40.8 14.7 %collective-permute-start.21 = (bf16[512,256]{1,0:T(8,128)(2,1)}, bf16[512,256]{1,0:T(8,128)(2,1)S(1)}, u32[]{:S(2)}, u32[]{:S(2)}) collective-permute-start(bf16[512,256]{1,0:T(8,128)(2,1)} %get-tuple-element.24), channel_id=1, source_target_pairs={{16,8},{8,16},{17,9},{9,17},{18,10},{10,18},{19,11},{11,19},{20,12... | collective-permute-start | bytes 786440 | tf_op jit(solution)/shard_map/ppermute | solution.py:235
  54.1 1.3 copy-start.15
  54.1 10.0 %collective-permute-start.20 = (bf16[512,256]{1,0:T(8,128)(2,1)}, bf16[512,256]{1,0:T(8,128)(2,1)}, u32[]{:S(2)}, u32[]{:S(2)}) collective-permute-start(bf16[512,256]{1,0:T(8,128)(2,1)} %get-tuple-element.24), channel_id=1, source_target_pairs={{16,0},{8,24},{17,1},{9,25},{18,2},{10,26},{19,3},{11,27},{20,4},{... | collective-permute-start | bytes 786440 | tf_op jit(solution)/shard_map/ppermute | solution.py:234
  55.5 0.7 copy-start.16
  55.5 22.7 %collective-permute-start.6 = (bf16[384,512]{1,0:T(8,128)(2,1)S(1)}, bf16[384,512]{1,0:T(8,128)(2,1)S(1)}, u32[]{:S(2)}, u32[]{:S(2)}) collective-permute-start(bf16[384,512]{1,0:T(8,128)(2,1)S(1)} %constant_dynamic-update-slice_fusion.refs_0_), channel_id=1, source_target_pairs={{0,1},{1,0},{2,3},{3,2},{4,5},{5,4},{6,7},{7,6},{8,9},{9,8},{10,11... | collective-permute-start | bytes 1179656 | tf_op jit(solution)/shard_map/ppermute | solution.py:150
  55.6 26.7 %copy-start.9 = (bf16[384,512]{1,0:T(8,128)(2,1)}, bf16[384,512]{1,0:T(8,128)(2,1)S(1)}, u32[]{:S(2)}) copy-start(bf16[384,512]{1,0:T(8,128)(2,1)S(1)} %collective-permute-done.11.refs_6_) | copy-start | bytes 1179652
  55.6 22.6 %collective-permute-start.12 = (bf16[384,512]{1,0:T(8,128)(2,1)S(1)}, bf16[384,512]{1,0:T(8,128)(2,1)}, u32[]{:S(2)}, u32[]{:S(2)}) collective-permute-start(bf16[384,512]{1,0:T(8,128)(2,1)S(1)} %collective-permute-done.11.refs_6_), channel_id=1, source_target_pairs={{0,1},{1,0},{2,3},{3,2},{4,5},{5,4},{6,7},{7,6},{8,9},{9,8},{10,11... | collective-permute-start | bytes 1179656 | tf_op jit(solution)/shard_map/ppermute | solution.py:150
  56.0 24.2 %collective-permute-start.10 = (bf16[384,512]{1,0:T(8,128)(2,1)}, bf16[384,512]{1,0:T(8,128)(2,1)}, u32[]{:S(2)}, u32[]{:S(2)}) collective-permute-start(bf16[384,512]{1,0:T(8,128)(2,1)} %collective-permute-done.9.refs_4_), channel_id=1, source_target_pairs={{0,1},{1,0},{2,3},{3,2},{4,5},{5,4},{6,7},{7,6},{8,9},{9,8},{10,11... | collective-permute-start | bytes 1179656 | tf_op jit(solution)/shard_map/ppermute | solution.py:150
  56.2 24.7 %collective-permute-start.8 = (bf16[384,512]{1,0:T(8,128)(2,1)}, bf16[384,512]{1,0:T(8,128)(2,1)}, u32[]{:S(2)}, u32[]{:S(2)}) collective-permute-start(bf16[384,512]{1,0:T(8,128)(2,1)} %collective-permute-done.7.refs_2_), channel_id=1, source_target_pairs={{0,1},{1,0},{2,3},{3,2},{4,5},{5,4},{6,7},{7,6},{8,9},{9,8},{10,11... | collective-permute-start | bytes 1179656 | tf_op jit(solution)/shard_map/ppermute | solution.py:150
  64.1 9.0 %collective-permute-start.15 = (bf16[528,256]{1,0:T(8,128)(2,1)}, bf16[528,256]{1,0:T(8,128)(2,1)}, u32[]{:S(2)}, u32[]{:S(2)}) collective-permute-start(bf16[528,256]{1,0:T(8,128)(2,1)} %get-tuple-element.20), channel_id=1, source_target_pairs={{0,24},{8,16},{16,8},{24,0},{1,25},{9,17},{17,9},{25,1},{2,26},{10... | collective-permute-start | bytes 811016 | tf_op jit(solution)/shard_map/ppermute | solution.py:150
  73.1 30.0 %collective-permute-start.14 = (bf16[528,256]{1,0:T(8,128)(2,1)}, bf16[528,256]{1,0:T(8,128)(2,1)}, u32[]{:S(2)}, u32[]{:S(2)}) collective-permute-start(bf16[528,256]{1,0:T(8,128)(2,1)} %get-tuple-element.20), channel_id=1, source_target_pairs={{0,16},{8,24},{16,0},{24,8},{1,17},{9,25},{17,1},{25,9},{2,18},{10... | collective-permute-start | bytes 811016 | tf_op jit(solution)/shard_map/ppermute | solution.py:150
  78.1 0.8 copy-start.10
  78.1 25.6 %collective-permute-start.13 = (bf16[528,256]{1,0:T(8,128)(2,1)}, bf16[528,256]{1,0:T(8,128)(2,1)}, u32[]{:S(2)}, u32[]{:S(2)}) collective-permute-start(bf16[528,256]{1,0:T(8,128)(2,1)} %get-tuple-element.20), channel_id=1, source_target_pairs={{0,8},{8,0},{16,24},{24,16},{1,9},{9,1},{17,25},{25,17},{2,10},{10... | collective-permute-start | bytes 811016 | tf_op jit(solution)/shard_map/ppermute | solution.py:150
  78.9 61.5 %collective-permute-start.16 = (bf16[1024,256]{1,0:T(8,128)(2,1)S(1)}, bf16[1024,256]{1,0:T(8,128)(2,1)S(1)}, u32[]{:S(2)}, u32[]{:S(2)}) collective-permute-start(bf16[1024,256]{1,0:T(8,128)(2,1)S(1)} %copy-done.4), channel_id=1, source_target_pairs={{0,8},{8,0},{16,24},{24,16},{1,9},{9,1},{17,25},{25,17},{2,10},{10... | collective-permute-start | bytes 1572872 | tf_op jit(solution)/shard_map/ppermute | solution.py:150
  80.2 37.8 %collective-permute-start.19 = (bf16[1024,256]{1,0:T(8,128)(2,1)S(1)}, bf16[1024,256]{1,0:T(8,128)(2,1)}, u32[]{:S(2)}, u32[]{:S(2)}) collective-permute-start(bf16[1024,256]{1,0:T(8,128)(2,1)S(1)} %copy-done.5), channel_id=1, source_target_pairs={{0,8},{8,0},{16,24},{24,16},{1,9},{9,1},{17,25},{25,17},{2,10},{10... | collective-permute-start | bytes 1572872 | tf_op jit(solution)/shard_map/ppermute | solution.py:150
  80.9 22.1 %copy-start.6 = (bf16[1024,256]{1,0:T(8,128)(2,1)S(1)}, bf16[1024,256]{1,0:T(8,128)(2,1)}, u32[]{:S(2)}) copy-start(bf16[1024,256]{1,0:T(8,128)(2,1)} %get-tuple-element.27) | copy-start | bytes 1572868
  80.9 81.8 %collective-permute-start.25 = (bf16[2048,256]{1,0:T(8,128)(2,1)}, bf16[2048,256]{1,0:T(8,128)(2,1)S(1)}, u32[]{:S(2)}, u32[]{:S(2)}) collective-permute-start(bf16[2048,256]{1,0:T(8,128)(2,1)} %get-tuple-element.26), channel_id=1, source_target_pairs={{0,8},{8,0},{16,24},{24,16},{1,9},{9,1},{17,25},{25,17},{2,10},{10... | collective-permute-start | bytes 3145736 | tf_op jit(solution)/shard_map/ppermute | solution.py:150
  103.1 59.6 %collective-permute-start.27 = (bf16[1024,256]{1,0:T(8,128)(2,1)S(1)}, bf16[1024,256]{1,0:T(8,128)(2,1)S(1)}, u32[]{:S(2)}, u32[]{:S(2)}) collective-permute-start(bf16[1024,256]{1,0:T(8,128)(2,1)S(1)} %copy-done.6), channel_id=1, source_target_pairs={{16,8},{8,16},{17,9},{9,17},{18,10},{10,18},{19,11},{11,19},{20,12... | collective-permute-start | bytes 1572872 | tf_op jit(solution)/shard_map/ppermute | solution.py:235
  103.8 58.9 %collective-permute-start.26 = (bf16[1024,256]{1,0:T(8,128)(2,1)S(1)}, bf16[1024,256]{1,0:T(8,128)(2,1)}, u32[]{:S(2)}, u32[]{:S(2)}) collective-permute-start(bf16[1024,256]{1,0:T(8,128)(2,1)S(1)} %copy-done.6), channel_id=1, source_target_pairs={{16,0},{8,24},{17,1},{9,25},{18,2},{10,26},{19,3},{11,27},{20,4},{... | collective-permute-start | bytes 1572872 | tf_op jit(solution)/shard_map/ppermute | solution.py:234
  118.1 22.3 %collective-permute-start.24 = (bf16[528,256]{1,0:T(8,128)(2,1)}, bf16[528,256]{1,0:T(8,128)(2,1)S(1)}, u32[]{:S(2)}, u32[]{:S(2)}) collective-permute-start(bf16[528,256]{1,0:T(8,128)(2,1)} %get-tuple-element.25), channel_id=1, source_target_pairs={{0,24},{8,16},{16,8},{24,0},{1,25},{9,17},{17,9},{25,1},{2,26},{10... | collective-permute-start | bytes 811016 | tf_op jit(solution)/shard_map/ppermute | solution.py:150
  118.1 22.3 %copy-start.11 = (bf16[528,256]{1,0:T(8,128)(2,1)S(1)}, bf16[528,256]{1,0:T(8,128)(2,1)}, u32[]{:S(2)}) copy-start(bf16[528,256]{1,0:T(8,128)(2,1)} %get-tuple-element.25) | copy-start | bytes 811012
  140.4 22.4 %copy-start.12 = (bf16[528,256]{1,0:T(8,128)(2,1)}, bf16[528,256]{1,0:T(8,128)(2,1)S(1)}, u32[]{:S(2)}) copy-start(bf16[528,256]{1,0:T(8,128)(2,1)S(1)} %collective-permute-done.24.refs_4_) | copy-start | bytes 811012
  140.4 16.1 %collective-permute-start.23 = (bf16[528,256]{1,0:T(8,128)(2,1)S(1)}, bf16[528,256]{1,0:T(8,128)(2,1)}, u32[]{:S(2)}, u32[]{:S(2)}) collective-permute-start(bf16[528,256]{1,0:T(8,128)(2,1)S(1)} %copy-done.11), channel_id=1, source_target_pairs={{0,16},{8,24},{16,0},{24,8},{1,17},{9,25},{17,1},{25,9},{2,18},{10... | collective-permute-start | bytes 811016 | tf_op jit(solution)/shard_map/ppermute | solution.py:150
  140.4 4.8 %copy-start.7 = (bf16[1024,256]{1,0:T(8,128)(2,1)}, bf16[1024,256]{1,0:T(8,128)(2,1)S(1)}, u32[]{:S(2)}) copy-start(bf16[1024,256]{1,0:T(8,128)(2,1)S(1)} %collective-permute-done.16.refs_5_) | copy-start | bytes 1572868
  140.4 22.3 %collective-permute-start.22 = (bf16[528,256]{1,0:T(8,128)(2,1)S(1)}, bf16[528,256]{1,0:T(8,128)(2,1)S(1)}, u32[]{:S(2)}, u32[]{:S(2)}) collective-permute-start(bf16[528,256]{1,0:T(8,128)(2,1)S(1)} %copy-done.11), channel_id=1, source_target_pairs={{0,8},{8,0},{16,24},{24,16},{1,9},{9,1},{17,25},{25,17},{2,10},{10... | collective-permute-start | bytes 811016 | tf_op jit(solution)/shard_map/ppermute | solution.py:150
  162.7 0.7 copy-start.13
  162.7 0.9 copy-start.8
  162.7 1.2 copy-start.3
  187.4 8.7 %copy-start = (f32[4,256,1024]{2,1,0:T(8,128)S(1)}, f32[4,256,1024]{2,1,0:T(8,128)}, u32[]{:S(2)}) copy-start(f32[4,256,1024]{2,1,0:T(8,128)} %get-tuple-element.30) | copy-start | bytes 12582916
  190.2 5.4 %collective-permute-start.30 = (f32[4]{0:T(128)S(1)}, f32[4]{0:T(128)S(1)}, u32[]{:S(2)}, u32[]{:S(2)}) collective-permute-start(f32[4]{0:T(128)S(1)} %multiply_reduce_fusion), channel_id=1, source_target_pairs={{0,24},{8,16},{16,8},{24,0},{1,25},{9,17},{17,9},{25,1},{2,26},{10... | collective-permute-start | bytes 56 | tf_op jit(solution)/shard_map/ppermute | solution.py:150
  190.7 4.8 %collective-permute-start.29 = (f32[4]{0:T(128)S(1)}, f32[4]{0:T(128)S(1)}, u32[]{:S(2)}, u32[]{:S(2)}) collective-permute-start(f32[4]{0:T(128)S(1)} %multiply_reduce_fusion), channel_id=1, source_target_pairs={{0,16},{8,24},{16,0},{24,8},{1,17},{9,25},{17,1},{25,9},{2,18},{10... | collective-permute-start | bytes 56 | tf_op jit(solution)/shard_map/ppermute | solution.py:150
  191.2 4.9 %collective-permute-start.28 = (f32[4]{0:T(128)S(1)}, f32[4]{0:T(128)S(1)}, u32[]{:S(2)}, u32[]{:S(2)}) collective-permute-start(f32[4]{0:T(128)S(1)} %multiply_reduce_fusion), channel_id=1, source_target_pairs={{0,8},{8,0},{16,24},{24,16},{1,9},{9,1},{17,25},{25,17},{2,10},{10... | collective-permute-start | bytes 56 | tf_op jit(solution)/shard_map/ppermute | solution.py:150
where the time goes:
time: 199 us
  Pallas kernels  75.4 us (38%)
  waiting for transfers between devices  71.2 us (36%)
  starting transfers between devices  41.2 us (21%)
  other arithmetic  7.05 us (4%)
  local copies, waits for them, and re-layouts  3 us (2%)
    ppermute x25, waiting for transfers between devices, pair_swap(): return lax.ppermute(value, axis, [(i, i ^ mask) for i in range(count)])  50.9 us
    pallas_call x3, Pallas kernels, chain(): pl.pallas_call(functools.partial(chain_body, first, blocks, applied is no...  46.1 us
    ppermute x25, starting transfers between devices, pair_swap(): return lax.ppermute(value, axis, [(i, i ^ mask) for i in range(count)])  35.3 us
    pallas_call x1, Pallas kernels, front(): pl.pallas_call(body, grid_spec=pltpu.PrefetchScalarGridSpec(num_scalar_pr...  20.8 us
    ppermute x3, waiting for transfers between devices, exchange(): skip = lax.ppermute(thin, 'tok', [(2, 0), (1, 3)])  20.2 us
    pallas_call x2, Pallas kernels, pack(): pl.pallas_call(functools.partial(pack_body, ranges), grid=(blocks,), in_s...  8.52 us
  transfers between devices with their start and end apart: 31, of which 9 were waited for; matrix products, arithmetic and copies ran while one was open for 1% of the time, Pallas kernels for 26%

commit v1 on v0

--- a/solution.py
+++ b/solution.py
@@ -192,15 +192,14 @@
     near = jnp.where(low, 2, 1)
     far = jnp.where(low, 3, 0)
     mate = jnp.where(me % 2 == 0, me + 1, me - 1)
-    for at, (start, size) in enumerate(ranges):
-        wide, thin = outs[2 * at], outs[2 * at + 1]
+    outs[-1][pl.ds(pl.multiple_of(b * tile, tile), tile), :] = tile_at(mate).astype(jnp.bfloat16)
+    for wide, (start, size) in zip(outs, ranges):
 
         @pl.when((b >= start) & (b < start + size))
         def _():
             slot = b - start
             wide[pl.ds(pl.multiple_of(slot * 2 * tile, tile), tile), :] = tile_at(near).astype(jnp.bfloat16)
             wide[pl.ds(pl.multiple_of(slot * 2 * tile + tile, tile), tile), :] = tile_at(far).astype(jnp.bfloat16)
-            thin[pl.ds(pl.multiple_of(slot * tile, tile), tile), :] = tile_at(mate).astype(jnp.bfloat16)
 
 
 def pack(roots, ranges):
@@ -208,7 +207,7 @@
     shapes = [jax.ShapeDtypeStruct((blocks * (tile // 2) + strip_rows(blocks), tile), jnp.bfloat16)]
     for _, size in ranges:
         shapes.append(jax.ShapeDtypeStruct((size * 2 * tile, tile), jnp.bfloat16))
-        shapes.append(jax.ShapeDtypeStruct((size * tile, tile), jnp.bfloat16))
+    shapes.append(jax.ShapeDtypeStruct((blocks * tile, tile), jnp.bfloat16))
     return pl.pallas_call(
         functools.partial(pack_body, ranges),
         grid=(blocks,),
@@ -222,41 +221,62 @@
     )(roots)
 
 
+def join_rows(arrays, pieces):
+    total = sum(stop - start for _, start, stop in pieces)
+    out = jax.ShapeDtypeStruct((total, arrays[0].shape[1]), arrays[0].dtype)
+
+    def body(*refs):
+        at = 0
+        for which, start, stop in pieces:
+            refs[-1][at : at + stop - start, :] = refs[which][start:stop, :]
+            at += stop - start
+
+    return pl.pallas_call(
+        body,
+        out_shape=out,
+        cost_estimate=pl.CostEstimate(flops=total, bytes_accessed=4 * total * out.shape[1], transcendentals=0),
+        compiler_params=pltpu.CompilerParams(vmem_limit_bytes=VMEM),
+    )(*arrays)
+
+
 def exchange(roots, ranges):
-    fold, *rest = pack(roots, ranges)
-    folds = []
-    for mask in (1, 2, 3):
-        folds.append(pair_swap(fold, "tok", mask))
-    parts = []
-    for at in range(len(ranges)):
-        wide, thin = rest[2 * at], rest[2 * at + 1]
-        wide = pair_swap(wide, "tok", 1)
-        skip = lax.ppermute(thin, "tok", [(2, 0), (1, 3)])
-        following = lax.ppermute(thin, "tok", [(2, 1), (1, 2)])
-        parts.append((wide, skip, following))
-    return folds, parts
-
-
-def front_body(place_ref, act, cot, left_gram, right_gram, left_root, pieces, left_next, right_next, applied, tokens, grad):
-    b = pl.program_id(0)
+    fold, *wides, thin = pack(roots, ranges)
+    cut = roots.shape[0] * roots.shape[1] // 2
+    mate = pair_swap(fold, "tok", 1)
+    arrived = []
+    for wide in wides:
+        arrived.append(pair_swap(wide, "tok", 1))
+    rows = fold.shape[0]
+    pieces = [(0, 0, thin.shape[0]), (1, 0, cut), (2, 0, cut), (1, cut, rows), (2, cut, rows)]
+    joined = join_rows([thin, fold, mate], pieces)
+    middle = lax.ppermute(joined, "tok", [(2, 1), (1, 2)])
+    outer = lax.ppermute(middle, "tok", [(1, 0), (2, 3)])
+    return arrived, (mate, middle, outer)
+
+
+def front_body(place_ref, act, cots, left_gram, right_gram, left_root, pieces, left_next, right_next, applied, tokens, cot, grad):
+    step = pl.program_id(0)
     rows, order = left_gram.shape[1:]
     group, width = act.shape[0], pieces[0].shape[1]
-    hid, first_row = place_ref[0], place_ref[1] * rows
-
-    @pl.when(b == 0)
-    def _():
-        tokens[:group, :] = act[...]
-        for mask, piece in enumerate(pieces):
-            column = jnp.bitwise_xor(hid, mask) * width
-            tokens[group:, pl.ds(pl.multiple_of(column, width), width)] = piece[...]
+    first_row = place_ref[1] * rows
+    odd = place_ref[0] % 2
+    tokens[:group, :] = act[...]
+    for at, one in enumerate(cots):
+        cot[at * group : (at + 1) * group, :] = one[...]
+    for at in range(len(pieces) // 2):
+
+        @pl.when(step == at)
+        def _():
+            tokens[group:, pl.ds(pl.multiple_of(odd * width, width), width)] = pieces[2 * at][...]
+            tokens[group:, pl.ds(pl.multiple_of((1 - odd) * width, width), width)] = pieces[2 * at + 1][...]
 
     both = (((0,), (0,)), ((), ()))
 
     @pl.loop(0, order // rows)
-    def _(step):
-        column = pl.multiple_of(b * order + step * rows, rows)
-        grad[pl.ds(pl.multiple_of(step * rows, rows), rows), :] = lax.dot_general(
-            tokens[:, pl.ds(column, rows)], cot[...], both, preferred_element_type=jnp.float32
+    def _(part):
+        chunk = pl.ds(pl.multiple_of(part * rows, rows), rows)
+        grad[chunk, :] = lax.dot_general(
+            tokens[:, chunk], cot[...], both, preferred_element_type=jnp.float32
         ).astype(jnp.bfloat16)
 
     slab = pl.ds(pl.multiple_of(first_row, rows), rows)
@@ -271,28 +291,44 @@
     ).astype(jnp.bfloat16)
 
 
-def front(place, act, cot, pieces, left_gram, right_gram, left_root):
+def front(place, act, cots, pieces, left_gram, right_gram, left_root, first, base):
     blocks, rows, order = left_gram.shape
     count = len(pieces)
-    depth = cot.shape[0]
-
-    def body(place_ref, act_ref, cot_ref, lg, rg, lr, *refs):
-        front_body(place_ref, act_ref, cot_ref, lg, rg, lr, refs[:count], *refs[count:])
+    groups = len(cots)
+    depth, width = groups * act.shape[0], cots[0].shape[1]
+    size = count // 2
+    held = 0 if base is None else len(base)
+
+    def body(place_ref, act_ref, lg, rg, lr, *refs):
+        cot_refs, refs = refs[:groups], refs[groups:]
+        front_body(place_ref, act_ref, cot_refs, lg, rg, lr, refs[:count], *refs[count + held :])
 
     def whole(array):
         return pl.BlockSpec(array.shape, lambda b, s: (0,) * array.ndim)
 
-    slab = pl.BlockSpec((1, rows, order), lambda b, s: (b, 0, 0))
+    def block_of(b, s):
+        return jnp.bitwise_xor(s[0] // 2, b + first)
+
+    slab = pl.BlockSpec((1, rows, order), lambda b, s: (block_of(b, s), 0, 0))
+    columns = pl.BlockSpec((act.shape[0], order), lambda b, s: (0, block_of(b, s)))
     shape = (blocks, rows, order)
+    operands = [place, act, left_gram, right_gram, left_root, *cots, *pieces]
+    specs = [columns, slab, slab, slab] + [whole(one) for one in (*cots, *pieces)]
+    aliases = {}
+    if base is not None:
+        aliases = {len(operands) + k: k for k in range(held)}
+        operands += base
+        specs += [pl.BlockSpec(memory_space=pl.ANY)] * held
     return pl.pallas_call(
         body,
         grid_spec=pltpu.PrefetchScalarGridSpec(
             num_scalar_prefetch=1,
-            grid=(blocks,),
-            in_specs=[whole(act), whole(cot), slab, slab, slab] + [whole(one) for one in pieces],
+            grid=(size,),
+            in_specs=specs,
             out_specs=[slab, slab, slab],
             scratch_shapes=[
-                pltpu.VMEM((depth, act.shape[1]), jnp.bfloat16),
+                pltpu.VMEM((depth, order), jnp.bfloat16),
+                pltpu.VMEM((depth, width), jnp.bfloat16),
                 pltpu.VMEM((order, order), jnp.bfloat16),
             ],
         ),
@@ -301,30 +337,37 @@
             jax.ShapeDtypeStruct(shape, jnp.float32),
             jax.ShapeDtypeStruct(shape, jnp.bfloat16),
         ],
+        input_output_aliases=aliases,
         cost_estimate=pl.CostEstimate(
-            flops=2 * blocks * order * order * (depth + 3 * rows),
-            bytes_accessed=blocks * rows * order * 22,
+            flops=2 * size * order * order * (depth + 3 * rows),
+            bytes_accessed=size * rows * order * 22,
             transcendentals=0,
         ),
         compiler_params=pltpu.CompilerParams(vmem_limit_bytes=VMEM),
-    )(place, act, cot, left_gram, right_gram, left_root, *pieces)
-
-
-def chain_body(first, total, with_update, with_base, *refs):
-    next_ref, root_ref, fold1, fold2, fold3, wide, skip, following = refs[:8]
-    refs = refs[8:]
+    )(*operands)
+
+
+def chain_body(first, total, with_update, with_base, with_scale, *refs):
+    next_ref, root_ref, wide, middle, outer, fold, strip_ref = refs[:7]
+    far_refs, refs = refs[7:15], refs[15:]
     if with_update:
         applied, refs = refs[0], refs[1:]
+    if with_scale:
+        scale_ref, unscaled, refs = refs[0], refs[1], refs[2:]
     if with_base:
         refs = refs[1:]
     refined, refs = refs[0], refs[1:]
+    if with_scale:
+        scaled, refs = refs[0], refs[1:]
+        many = unscaled.shape[0]
+        for at in range(many):
+            scaled[at] = unscaled[at] * scale_ref[pl.program_id(0) * many + at]
     if with_update:
-        precond, refs = refs[0], refs[1:]
+        precond, energy, refs = refs[0], refs[1], refs[2:]
     full, product = refs
     tile = root_ref.shape[1]
     half = tile // 2
-    slot = pl.program_id(0)
-    b = slot + first
+    b = pl.program_id(0) + first
     me = lax.axis_index("tok")
     low = me < 2
     end = (me == 0) | (me == 3)
@@ -344,14 +387,11 @@
     row, column = diagonal_masks(half)
     strip = strip_rows(total)
     line = lax.broadcasted_iota(jnp.int32, (strip, half), 0)
-    place = pl.ds(pl.multiple_of(b * half, half), half)
-
-    def unfold(index, fold):
-        folded = fold[place, :half].astype(jnp.float32)
-        corner = fold[place, half:]
+
+    def unfold(index, folded, corner, held):
+        folded, held = folded.astype(jnp.float32), held.astype(jnp.float32)
         turned = folded.T
-        strips = fold[pl.ds(total * half, strip), :half].astype(jnp.float32)
-        diagonal = jnp.sum(jnp.where(line == b, strips, 0.0), axis=0, keepdims=True)
+        diagonal = jnp.sum(jnp.where(line == b, held, 0.0), axis=0, keepdims=True)
         full[at(index, 0, half), at(index, 0, half)] = jnp.where(row <= column, folded, turned).astype(jnp.bfloat16)
         lower = jnp.where(row == column, diagonal, jnp.where(row > column, folded, turned))
         full[at(index, half, half), at(index, half, half)] = lower.astype(jnp.bfloat16)
@@ -362,19 +402,23 @@
         full[at(i), at(j)] = value
         full[at(j), at(i)] = flipped(value)
 
-    unfold(mate, fold1)
-    unfold(jnp.where(low, me + 2, me - 2), fold2)
-    unfold(3 - me, fold3)
-    both(mate, near, wide[pl.ds(pl.multiple_of(slot * 2 * tile, tile), tile), :])
-    both(mate, far, wide[pl.ds(pl.multiple_of(slot * 2 * tile + tile, tile), tile), :])
-    thin = pl.ds(pl.multiple_of(slot * tile, tile), tile)
-    both(near, far, jnp.where(end, skip[thin, :], following[thin, :]))
+    def arrived(k, columns):
+        return jnp.where(end, far_refs[k + 4][:, columns], far_refs[k][:, columns])
+
+    left, right = slice(0, half), slice(half, tile)
+    unfold(mate, fold[:, left], fold[:, right], strip_ref[:, left])
+    unfold(near, arrived(0, left), arrived(0, right), arrived(1, left))
+    unfold(far, arrived(2, left), arrived(2, right), arrived(3, left))
+    both(mate, near, wide[:tile, :])
+    both(mate, far, wide[tile:, :])
+    both(near, far, jnp.where(end, outer[...], middle[...]))
     if with_update:
-        precond[0] = jnp.dot(applied[0], full[...], preferred_element_type=jnp.float32)
+        value = jnp.dot(applied[0], full[...], preferred_element_type=jnp.float32)
+        precond[0] = value
+        energy[0] = jnp.sum((value * value).reshape(-1, 8, value.shape[1]), axis=0)
     product[...] = next_ref[0].astype(jnp.bfloat16)
 
-    @pl.loop(0, 4)
-    def _(repeat):
+    for _ in range(4):
         product[...] = jnp.dot(
             product[...], full[...], preferred_element_type=jnp.float32
         ).astype(jnp.bfloat16)
@@ -383,33 +427,57 @@
     refined[0] = (5.0 * root_ref[0] - final) / 4.0
 
 
-def chain(next_rows, roots, folds, tiles, applied, base, first, size):
+def chain(next_rows, roots, wide, messages, applied, base, first, size, scaling=None):
     blocks, rows, order = roots.shape
 
     def slab(array):
         return pl.BlockSpec((1,) + array.shape[1:], lambda b: (b + first, 0, 0))
 
-    def whole(array):
-        return pl.BlockSpec(array.shape, lambda b: (0, 0))
-
-    operands = [next_rows, roots, *folds, *tiles]
-    specs = [slab(next_rows), slab(roots)] + [whole(one) for one in (*folds, *tiles)]
+    half, strip = rows // 2, strip_rows(blocks)
+
+    def fold_specs(offset, slots):
+        def folded(slot):
+            start = (offset + slot * blocks * half) // half
+            return pl.BlockSpec((half, rows), lambda b: (b + first + start, 0))
+
+        def diagonal(slot):
+            start = (offset + slots * blocks * half) // strip + slot
+            return pl.BlockSpec((strip, rows), lambda b: (start, 0))
+
+        return [spec for slot in range(slots) for spec in (folded(slot), diagonal(slot))]
+
+    fold, middle, outer = messages
+    offset = blocks * rows
+    operands = [next_rows, roots, wide, middle, outer, fold, fold] + [middle] * 4 + [outer] * 4
+    specs = [slab(next_rows), slab(roots), pl.BlockSpec((2 * rows, rows), lambda b: (b, 0))]
+    specs += [pl.BlockSpec((rows, rows), lambda b: (b + first, 0))] * 2
+    specs += fold_specs(0, 1) + fold_specs(offset, 2) * 2
     if applied is not None:
         operands.append(applied)
         specs.append(slab(applied))
     aliases = {}
+    if scaling is not None:
+        operands += scaling
+        share = pl.BlockSpec((blocks // size, rows, order), lambda b: (b, 0, 0))
+        specs += [pl.BlockSpec(memory_space=pltpu.SMEM), share]
     if base is not None:
         aliases = {len(operands): 0}
         operands.append(base)
         specs.append(pl.BlockSpec(memory_space=pl.ANY))
     out = jax.ShapeDtypeStruct((blocks, rows, order), jnp.float32)
-    outputs = [out] if applied is None else [out, out]
+    outputs = [out] if applied is None else [out, out, jax.ShapeDtypeStruct((blocks, 8, order), jnp.float32)]
+    out_specs = [slab(one) for one in outputs]
+    if scaling is not None:
+        outputs.append(out)
+        out_specs.append(share)
     matmuls = 5 if applied is None else 6
     return pl.pallas_call(
-        functools.partial(chain_body, first, blocks, applied is not None, base is not None),
+        functools.partial(
+            chain_body, first, blocks, applied is not None, base is not None, scaling is not None
+        ),
         grid=(size,),
         in_specs=specs,
-        out_specs=[slab(one) for one in outputs],
+        out_specs=out_specs,
         out_shape=outputs,
         input_output_aliases=aliases,
         scratch_shapes=[
@@ -435,14 +503,14 @@
         arrived.append(pair_swap(piece, "tok", mask))
     for mask in (1, 2, 3):
         cots.append(pair_swap(cotangent, "tok", mask))
-    mine = jnp.concatenate(arrived, axis=0)
+    mine = join_rows(arrived, [(at, 0, one.shape[0]) for at, one in enumerate(arrived)])
     held = [mine]
     for mask in range(2, count, 2):
         held.append(pair_swap(mine, "hid", mask))
     pieces = []
     for one in held:
         pieces += [one, pair_swap(one, "hid", 1)]
-    return pieces, jnp.concatenate(cots, axis=0)
+    return pieces, cots
 
 
 def line_program(activations, cotangent, left_gram, right_gram, left_root, right_root):
@@ -450,27 +518,34 @@
     right_ranges = part_ranges(RIGHT_PARTS, blocks)
     left_ranges = part_ranges(LEFT_PARTS, blocks)
     pieces, cots = gather_tokens(activations, cotangent)
-    right_folds, right_tiles = exchange(right_root, right_ranges)
-    left_folds, left_tiles = exchange(left_root, left_ranges)
+    right_wide, right_messages = exchange(right_root, right_ranges)
+    left_wide, left_messages = exchange(left_root, left_ranges)
     place = jnp.stack([lax.axis_index("hid"), lax.axis_index("tok")]).astype(jnp.int32)
-    left_next, right_next, applied = front(
-        place, activations, cots, pieces, left_gram, right_gram, left_root
-    )
+    base = None
+    share = max(2, len(pieces) // 2)
+    for at in range(0, len(pieces), share):
+        base = front(
+            place, activations, cots, pieces[at : at + share],
+            left_gram, right_gram, left_root, at // 2, base,
+        )
+    left_next, right_next, applied = base
     (first, size), = right_ranges
-    right_refined, precond = chain(
-        right_next, right_root, right_folds, right_tiles[0], applied, None, first, size
-    )
-    local = jnp.sum(precond * precond, axis=(1, 2))
+    right_refined, precond, energy = chain(
+        right_next, right_root, right_wide[0], right_messages, applied, None, first, size
+    )
+    local = jnp.sum(energy, axis=(1, 2))
     squares = local
     for mask in (1, 2, 3):
         squares = squares + pair_swap(local, "tok", mask)
-    scale = jnp.sqrt(squares / (order * order) + EPS)
-    update = precond / scale[:, None, None]
-    left_refined = None
+    scale = 1.0 / jnp.sqrt(squares / (order * order) + EPS)
+    left_refined = update = None
     for at, (first, size) in enumerate(left_ranges):
-        (left_refined,) = chain(
-            left_next, left_root, left_folds, left_tiles[at], None, left_refined, first, size
+        last = at == len(left_ranges) - 1 and blocks % size == 0
+        left_refined, *update = chain(
+            left_next, left_root, left_wide[at], left_messages, None, left_refined,
+            first, size, [scale, precond] if last else None
         )
+    update = update[0] if update else precond * scale[:, None, None]
     return left_next, right_next, left_refined, right_refined, update
 
 
@@ -496,8 +571,9 @@
         tok, hid = mesh.shape["tok"], mesh.shape["hid"]
         whole_blocks = cotangent[1] == left_gram[2]
         one_column = left_gram[0] == activations[1] // left_gram[2]
-        even = hid >= 2 and hid & (hid - 1) == 0
-        if tok == 4 and whole_blocks and one_column and even:
+        even = hid >= 4 and hid & (hid - 1) == 0
+        halves = 2 * left_gram[0] == hid
+        if tok == 4 and whole_blocks and one_column and even and halves:
             return line_program(*operands)
         return on_device(*operands)
 

time: 199 us -> 213 us (1.070)
  waiting for transfers between devices: 71.2 us -> 92.6 us
  starting transfers between devices: 41.2 us -> 31.4 us
  Pallas kernels: 75.4 us -> 80.9 us
  other arithmetic: 7.05 us -> 2.21 us
    ppermute x25 -> x21, waiting for transfers between devices: 50.9 us -> 63.8 us  [pair_swap(): return lax.ppermute(value, axis, [(i, i ^ mask) for i in range(count)])]
    ppermute x25 -> x21, starting transfers between devices: 35.3 us -> 26.2 us  [pair_swap(): return lax.ppermute(value, axis, [(i, i ^ mask) for i in range(count)])]
    ppermute x6 -> x4, waiting for transfers between devices: 20.2 us -> 28.8 us  [the longest x2 28.8 us: exchange(): outer = lax.ppermute(middle, 'tok', [(1, 0), (2, 3)])]
    pallas_call x0 -> x3, Pallas kernels: none -> 6.39 us  [join_rows(): pl.pallas_call(body, out_shape=out, cost_estimate=pl.CostEstimate(flops=t...]
    pallas_call x3, Pallas kernels: 46.1 us -> 40.6 us  [chain(): pl.pallas_call(functools.partial(chain_body, first, blocks, applied is no...]
    pallas_call x1 -> x2, Pallas kernels: 20.8 us -> 25.3 us  [front(): pl.pallas_call(body, grid_spec=pltpu.PrefetchScalarGridSpec(num_scalar_pr...]
    div x1 -> x0, other arithmetic: 2.59 us -> none  [line_program(): update = precond / scale[:, None, None]]
    ppermute x6 -> x4, starting transfers between devices: 5.89 us -> 5.15 us  [the longest x2 2.76 us: exchange(): outer = lax.ppermute(middle, 'tok', [(1, 0), (2, 3)])]
  transfers between devices with their start and end apart: 31 -> 25, of which waited for: 9 -> 10; matrix products, arithmetic and copies ran while one was open for 1% -> 1% of each run, Pallas kernels for 26% -> 30%
where the time goes in v1:
time: 213 us
  waiting for transfers between devices  92.6 us (43%)
  Pallas kernels  80.9 us (38%)
  starting transfers between devices  31.4 us (15%)
  local copies, waits for them, and re-layouts  4.8 us (2%)
  other arithmetic  2.21 us (1%)
    ppermute x21, waiting for transfers between devices, pair_swap(): return lax.ppermute(value, axis, [(i, i ^ mask) for i in range(count)])  63.8 us
    pallas_call x3, Pallas kernels, chain(): pl.pallas_call(functools.partial(chain_body, first, blocks, applied is no...  40.6 us
    ppermute x2, waiting for transfers between devices, exchange(): outer = lax.ppermute(middle, 'tok', [(1, 0), (2, 3)])  28.8 us
    ppermute x21, starting transfers between devices, pair_swap(): return lax.ppermute(value, axis, [(i, i ^ mask) for i in range(count)])  26.2 us
    pallas_call x2, Pallas kernels, front(): pl.pallas_call(body, grid_spec=pltpu.PrefetchScalarGridSpec(num_scalar_pr...  25.3 us
    pallas_call x2, Pallas kernels, pack(): pl.pallas_call(functools.partial(pack_body, ranges), grid=(blocks,), in_s...  8.57 us
    pallas_call x3, Pallas kernels, join_rows(): pl.pallas_call(body, out_shape=out, cost_estimate=pl.CostEstimate(flops=t...  6.39 us
  transfers between devices with their start and end apart: 25, of which 10 were waited for; matrix products, arithmetic and copies ran while one was open for 1% of the time, Pallas kernels for 30%

profile of v1, /device:TPU:0, one launch (start us, length us, event | category | flops | bytes accessed | tf_op | source)
XLA Modules:
  0.0 212.9 jit_solution(12754282987632074250)
XLA Ops:
  0.6 0.0 copy-start.11
  0.6 4.3 %shard_map.106 = (bf16[528,256]{1,0:T(8,128)(2,1)}, bf16[2048,256]{1,0:T(8,128)(2,1)}, bf16[1024,256]{1,0:T(8,128)(2,1)}) custom-call(f32[4,256,1024]{2,1,0:T(8,128)} %refs_1_.3), custom_call_target="tpu_custom_call" | custom-call | flops 2097152 | bytes 6291456 | tf_op jit(solution)/shard_map/pallas_call | solution.py:211
  4.9 3.1 %collective-permute-start.18 = (bf16[528,256]{1,0:T(8,128)(2,1)}, bf16[528,256]{1,0:T(8,128)(2,1)S(1)}, u32[]{:S(2)}, u32[]{:S(2)}) collective-permute-start(bf16[528,256]{1,0:T(8,128)(2,1)} %get-tuple-element.33.refs_1_), channel_id=1, source_target_pairs={{0,8},{8,0},{16,24},{24,16},{1,9},{9,1},{17,25},{25,17},{2,10},{10... | collective-permute-start | bytes 811016 | tf_op jit(solution)/shard_map/ppermute | solution.py:150
  8.0 6.7 %collective-permute-done.18.refs_2_.refs_5_.refs_6_ = bf16[528,256]{1,0:T(8,128)(2,1)S(1)} collective-permute-done((bf16[528,256]{1,0:T(8,128)(2,1)}, bf16[528,256]{1,0:T(8,128)(2,1)S(1)}, u32[]{:S(2)}, u32[]{:S(2)}) %collective-permute-start.18) | collective-permute-done | bytes 270368 | tf_op jit(solution)/shard_map/ppermute | solution.py:150
  14.7 0.7 copy-done.10
  15.4 2.3 %shard_map.107 = bf16[2080,256]{1,0:T(8,128)(2,1)} custom-call(bf16[1024,256]{1,0:T(8,128)(2,1)} %get-tuple-element.32.refs_0_, bf16[528,256]{1,0:T(8,128)(2,1)} %get-tuple-element.33.refs_1_, bf16[528,256]{1,0:T(8,128)(2,1)} %copy-done.10), custom_call_target="tpu_custom_call" | custom-call | flops 2080 | bytes 2129920 | tf_op jit(solution)/shard_map/pallas_call | solution.py:234
  17.7 1.7 collective-permute-start.19
  19.3 3.8 %collective-permute-start.2 = (bf16[128,1024]{1,0:T(8,128)(2,1)S(1)}, bf16[128,1024]{1,0:T(8,128)(2,1)S(1)}, u32[]{:S(2)}, u32[]{:S(2)}) collective-permute-start(bf16[128,1024]{1,0:T(8,128)(2,1)S(1)} %copy-done.11), channel_id=1, source_target_pairs={{0,24},{8,16},{16,8},{24,0},{1,25},{9,17},{17,9},{25,1},{2,26},{10... | collective-permute-start | bytes 786440 | tf_op jit(solution)/shard_map/ppermute | solution.py:150
  23.1 0.9 constant_dynamic-slice_fusion
  24.0 0.1 collective-permute-start.5
  24.1 1.7 collective-permute-start.4
  25.9 2.6 %collective-permute-start.3 = (bf16[128,512]{1,0:T(8,128)(2,1)S(1)}, bf16[128,512]{1,0:T(8,128)(2,1)S(1)}, u32[]{:S(2)}, u32[]{:S(2)}) collective-permute-start(bf16[128,512]{1,0:T(8,128)(2,1)S(1)} %constant_dynamic-slice_fusion), channel_id=1, source_target_pairs={{0,8},{8,0},{16,24},{24,16},{1,9},{9,1},{17,25},{25,17},{2,10},{10... | collective-permute-start | bytes 393224 | tf_op jit(solution)/shard_map/ppermute | solution.py:150
  28.5 4.5 %collective-permute-done.5.refs_2_ = bf16[128,512]{1,0:T(8,128)(2,1)S(1)} collective-permute-done((bf16[128,512]{1,0:T(8,128)(2,1)S(1)}, bf16[128,512]{1,0:T(8,128)(2,1)S(1)}, u32[]{:S(2)}, u32[]{:S(2)}) %collective-permute-start.5) | collective-permute-done | bytes 131104 | tf_op jit(solution)/shard_map/ppermute | solution.py:150
  33.0 34.8 %collective-permute-done.4.refs_1_ = bf16[128,512]{1,0:T(8,128)(2,1)S(1)} collective-permute-done((bf16[128,512]{1,0:T(8,128)(2,1)S(1)}, bf16[128,512]{1,0:T(8,128)(2,1)S(1)}, u32[]{:S(2)}, u32[]{:S(2)}) %collective-permute-start.4) | collective-permute-done | bytes 131104 | tf_op jit(solution)/shard_map/ppermute | solution.py:150
  67.8 0.0 collective-permute-done.3.refs_0_
  67.8 0.6 copy-done.16
  68.5 0.7 copy-done.17
  69.1 1.8 shard_map.101.refs_4_
  70.9 1.5 collective-permute-start.11
  72.4 0.2 collective-permute-start.1
  72.6 2.8 %collective-permute-start = (bf16[128,1024]{1,0:T(8,128)(2,1)S(1)}, bf16[128,1024]{1,0:T(8,128)(2,1)S(1)}, u32[]{:S(2)}, u32[]{:S(2)}) collective-permute-start(bf16[128,1024]{1,0:T(8,128)(2,1)S(1)} %copy-done.11), channel_id=1, source_target_pairs={{0,8},{8,0},{16,24},{24,16},{1,9},{9,1},{17,25},{25,17},{2,10},{10... | collective-permute-start | bytes 786440 | tf_op jit(solution)/shard_map/ppermute | solution.py:150
  75.5 4.3 %shard_map.104 = (bf16[528,256]{1,0:T(8,128)(2,1)}, bf16[1024,256]{1,0:T(8,128)(2,1)}, bf16[1024,256]{1,0:T(8,128)(2,1)}, bf16[1024,256]{1,0:T(8,128)(2,1)}) custom-call(f32[4,256,1024]{2,1,0:T(8,128)} %refs_1_.5), custom_call_target="tpu_custom_call" | custom-call | flops 2097152 | bytes 6291456 | tf_op jit(solution)/shard_map/pallas_call | solution.py:211
  79.7 0.0 collective-permute-done.2.refs_3_
  79.7 0.0 collective-permute-start.14
  79.8 5.3 %collective-permute-done.1.refs_2_ = bf16[128,1024]{1,0:T(8,128)(2,1)S(1)} collective-permute-done((bf16[128,1024]{1,0:T(8,128)(2,1)S(1)}, bf16[128,1024]{1,0:T(8,128)(2,1)S(1)}, u32[]{:S(2)}, u32[]{:S(2)}) %collective-permute-start.1) | collective-permute-done | bytes 262176 | tf_op jit(solution)/shard_map/ppermute | solution.py:150
  85.0 0.0 collective-permute-start.10
  85.0 2.2 %collective-permute-done.refs_1_ = bf16[128,1024]{1,0:T(8,128)(2,1)S(1)} collective-permute-done((bf16[128,1024]{1,0:T(8,128)(2,1)S(1)}, bf16[128,1024]{1,0:T(8,128)(2,1)S(1)}, u32[]{:S(2)}, u32[]{:S(2)}) %collective-permute-start) | collective-permute-done | bytes 262176 | tf_op jit(solution)/shard_map/ppermute | solution.py:150
  87.2 1.5 collective-permute-start.8
  88.7 2.6 %collective-permute-done.14.refs_2_.refs_5_.refs_6_ = bf16[528,256]{1,0:T(8,128)(2,1)S(1)} collective-permute-done((bf16[528,256]{1,0:T(8,128)(2,1)}, bf16[528,256]{1,0:T(8,128)(2,1)S(1)}, u32[]{:S(2)}, u32[]{:S(2)}) %collective-permute-start.14) | collective-permute-done | bytes 270368 | tf_op jit(solution)/shard_map/ppermute | solution.py:150
  91.4 1.5 collective-permute-start.6
  92.9 0.0 collective-permute-done.11.refs_6_
  92.9 0.1 collective-permute-start.12
  93.0 2.3 %shard_map.105 = bf16[2080,256]{1,0:T(8,128)(2,1)} custom-call(bf16[1024,256]{1,0:T(8,128)(2,1)} %get-tuple-element.29.refs_0_, bf16[528,256]{1,0:T(8,128)(2,1)} %get-tuple-element.30.refs_1_, bf16[528,256]{1,0:T(8,128)(2,1)} %copy-done.2), custom_call_target="tpu_custom_call" | custom-call | flops 2080 | bytes 2129920 | tf_op jit(solution)/shard_map/pallas_call | solution.py:234
  95.3 0.0 collective-permute-done.10.refs_5_
  95.3 0.3 collective-permute-start.17
  95.6 2.0 collective-permute-done.8.refs_6_
  97.6 0.7 collective-permute-start.15
  98.3 1.3 collective-permute-start.20
  99.6 0.6 pad_add_fusion.place_ref
  100.2 5.7 %collective-permute-done.6.refs_4_ = bf16[384,512]{1,0:T(8,128)(2,1)S(1)} collective-permute-done((bf16[384,512]{1,0:T(8,128)(2,1)S(1)}, bf16[384,512]{1,0:T(8,128)(2,1)S(1)}, u32[]{:S(2)}, u32[]{:S(2)}) %collective-permute-start.6) | collective-permute-done | bytes 393248 | tf_op jit(solution)/shard_map/ppermute | solution.py:150
  105.9 0.1 collective-permute-start.9
  106.0 0.0 collective-permute-done.12.refs_7_
  106.0 0.4 collective-permute-start.7
  106.4 12.7 %shard_map.102 = (f32[4,256,1024]{2,1,0:T(8,128)}, f32[4,256,1024]{2,1,0:T(8,128)}, bf16[4,256,1024]{2,1,0:T(8,128)(2,1)}) custom-call(s32[2]{0:T(128)} %pad_add_fusion.place_ref, bf16[128,4096]{1,0:T(8,128)(2,1)} %act_ref.3, f32[4,256,1024]{2,1,0:T(8,128)} %lg.3, f32[4,256,1024]{2,1,0:T(8,128)} %rg.3, f32[4,256,1024]{2,1,0:T(8,128)} %refs_1_.5, ...), custom_call_target="tpu_custom_call" | custom-call | flops 5368709120 | bytes 11534336 | tf_op jit(solution)/shard_map/pallas_call | solution.py:322
  119.1 0.0 collective-permute-done.9.refs_7_
  119.1 0.1 collective-permute-start.13
  119.2 0.0 collective-permute-done.7.refs_5_
  119.2 2.0 collective-permute-start.24
  121.2 12.7 %shard_map.103 = (f32[4,256,1024]{2,1,0:T(8,128)}, f32[4,256,1024]{2,1,0:T(8,128)}, bf16[4,256,1024]{2,1,0:T(8,128)(2,1)}) custom-call(s32[2]{0:T(128)} %pad_add_fusion.place_ref, bf16[128,4096]{1,0:T(8,128)(2,1)} %act_ref.3, f32[4,256,1024]{2,1,0:T(8,128)} %lg.3, f32[4,256,1024]{2,1,0:T(8,128)} %rg.3, ...), custom_call_target="tpu_custom_call", output_to_operand_aliasing={{0}: (13, {}), {1}: (14, {}), {2}: (15, {})} | custom-call | flops 5368709120 | bytes 11534336 | tf_op jit(solution)/shard_map/pallas_call | solution.py:322
  133.9 0.0 collective-permute-done.15.refs_3_.refs_7_.refs_8_.refs_9_.refs_10_
  133.9 1.5 collective-permute-start.16
  135.4 9.1 %collective-permute-done.20.refs_4_.refs_11_.refs_12_.refs_13_.refs_14_ = bf16[2080,256]{1,0:T(8,128)(2,1)} collective-permute-done((bf16[2080,256]{1,0:T(8,128)(2,1)}, bf16[2080,256]{1,0:T(8,128)(2,1)}, u32[]{:S(2)}, u32[]{:S(2)}) %collective-permute-start.20) | collective-permute-done | bytes 1064992 | tf_op jit(solution)/shard_map/ppermute | solution.py:253
  144.5 19.4 %shard_map.108 = (f32[4,256,1024]{2,1,0:T(8,128)}, f32[4,256,1024]{2,1,0:T(8,128)}, f32[4,8,1024]{2,1,0:T(8,128)}) custom-call(f32[4,256,1024]{2,1,0:T(8,128)} %get-tuple-element.19.refs_0_, f32[4,256,1024]{2,1,0:T(8,128)} %refs_1_.3, bf16[2048,256]{1,0:T(8,128)(2,1)} %collective-permute-done.17.refs_2_, ...), custom_call_target="tpu_custom_call" | custom-call | flops 12884901888 | bytes 20971520 | tf_op jit(solution)/shard_map/pallas_call | solution.py:474
  163.9 1.0 reduce_sum.9
  164.9 2.3 %collective-permute-start.23 = (f32[4]{0:T(128)S(1)}, f32[4]{0:T(128)S(1)}, u32[]{:S(2)}, u32[]{:S(2)}) collective-permute-start(f32[4]{0:T(128)S(1)} %reduce_sum.9), channel_id=1, source_target_pairs={{0,24},{8,16},{16,8},{24,0},{1,25},{9,17},{17,9},{25,1},{2,26},{10... | collective-permute-start | bytes 56 | tf_op jit(solution)/shard_map/ppermute | solution.py:150
  167.2 2.2 %collective-permute-start.21 = (f32[4]{0:T(128)S(1)}, f32[4]{0:T(128)S(1)}, u32[]{:S(2)}, u32[]{:S(2)}) collective-permute-start(f32[4]{0:T(128)S(1)} %reduce_sum.9), channel_id=1, source_target_pairs={{0,8},{8,0},{16,24},{24,16},{1,9},{9,1},{17,25},{25,17},{2,10},{10... | collective-permute-start | bytes 56 | tf_op jit(solution)/shard_map/ppermute | solution.py:150
  169.4 19.8 %collective-permute-done.16.refs_4_.refs_11_.refs_12_.refs_13_.refs_14_ = bf16[2080,256]{1,0:T(8,128)(2,1)S(1)} collective-permute-done((bf16[2080,256]{1,0:T(8,128)(2,1)S(1)}, bf16[2080,256]{1,0:T(8,128)(2,1)S(1)}, u32[]{:S(2)}, u32[]{:S(2)}) %collective-permute-start.16) | collective-permute-done | bytes 1064992 | tf_op jit(solution)/shard_map/ppermute | solution.py:253
  189.1 1.0 copy-done.1
  190.1 9.7 %shard_map.109.refs_17_ = f32[4,256,1024]{2,1,0:T(8,128)} custom-call(f32[4,256,1024]{2,1,0:T(8,128)} %get-tuple-element.18.refs_0_, f32[4,256,1024]{2,1,0:T(8,128)} %refs_1_.5, bf16[1024,256]{1,0:T(8,128)(2,1)} %copy-done.4, bf16[2080,256]{1,0:T(8,128)(2,1)} %copy-done, bf16[2080,256]{1,0:T(8,128)(2,1)} %copy-done.1, bf16[528,256]{1,0:T(8,128)(2,1)} %copy-done.2, ...), custom_call_target="tpu_custom_call" | custom-call | flops 5368709120 | bytes 10485760 | tf_op jit(solution)/shard_map/pallas_call | solution.py:474
  199.9 0.0 collective-permute-done.23
  199.9 0.0 collective-permute-done.22
  199.9 0.6 add_rsqrt_fusion.refs_15_
  200.5 0.8 copy-done.3
  201.3 11.4 %shard_map.110 = (f32[4,256,1024]{2,1,0:T(8,128)}, f32[4,256,1024]{2,1,0:T(8,128)}) custom-call(f32[4,256,1024]{2,1,0:T(8,128)} %get-tuple-element.18.refs_0_, f32[4,256,1024]{2,1,0:T(8,128)} %refs_1_.5, bf16[1024,256]{1,0:T(8,128)(2,1)} %copy-done.3, bf16[2080,256]{1,0:T(8,128)(2,1)} %copy-done, ...), custom_call_target="tpu_custom_call", output_to_operand_aliasing={{0}: (17, {})} | custom-call | flops 5368709120 | bytes 10485760 | tf_op jit(solution)/shard_map/pallas_call | solution.py:474
  (40 shorter events, 0.1 us)
Async XLA Ops:
  0.6 18.7 %copy-start.11 = (bf16[128,1024]{1,0:T(8,128)(2,1)S(1)}, bf16[128,1024]{1,0:T(8,128)(2,1)}, u32[]{:S(2)}) copy-start(bf16[128,1024]{1,0:T(8,128)(2,1)} %refs_0_.3) | copy-start | bytes 786436
  4.9 9.7 %collective-permute-start.18 = (bf16[528,256]{1,0:T(8,128)(2,1)}, bf16[528,256]{1,0:T(8,128)(2,1)S(1)}, u32[]{:S(2)}, u32[]{:S(2)}) collective-permute-start(bf16[528,256]{1,0:T(8,128)(2,1)} %get-tuple-element.33.refs_1_), channel_id=1, source_target_pairs={{0,8},{8,0},{16,24},{24,16},{1,9},{9,1},{17,25},{25,17},{2,10},{10... | collective-permute-start | bytes 811016 | tf_op jit(solution)/shard_map/ppermute | solution.py:150
  14.7 0.7 copy-start.10
  17.7 80.6 %collective-permute-start.19 = (bf16[2080,256]{1,0:T(8,128)(2,1)}, bf16[2080,256]{1,0:T(8,128)(2,1)}, u32[]{:S(2)}, u32[]{:S(2)}) collective-permute-start(bf16[2080,256]{1,0:T(8,128)(2,1)} %shard_map.107), channel_id=1, source_target_pairs={{16,8},{8,16},{17,9},{9,17},{18,10},{10,18},{19,11},{11,19},{20,12... | collective-permute-start | bytes 3194888 | tf_op jit(solution)/shard_map/ppermute | solution.py:252
  19.3 60.4 %collective-permute-start.2 = (bf16[128,1024]{1,0:T(8,128)(2,1)S(1)}, bf16[128,1024]{1,0:T(8,128)(2,1)S(1)}, u32[]{:S(2)}, u32[]{:S(2)}) collective-permute-start(bf16[128,1024]{1,0:T(8,128)(2,1)S(1)} %copy-done.11), channel_id=1, source_target_pairs={{0,24},{8,16},{16,8},{24,0},{1,25},{9,17},{17,9},{25,1},{2,26},{10... | collective-permute-start | bytes 786440 | tf_op jit(solution)/shard_map/ppermute | solution.py:150
  24.0 9.0 %collective-permute-start.5 = (bf16[128,512]{1,0:T(8,128)(2,1)S(1)}, bf16[128,512]{1,0:T(8,128)(2,1)S(1)}, u32[]{:S(2)}, u32[]{:S(2)}) collective-permute-start(bf16[128,512]{1,0:T(8,128)(2,1)S(1)} %constant_dynamic-slice_fusion), channel_id=1, source_target_pairs={{0,24},{8,16},{16,8},{24,0},{1,25},{9,17},{17,9},{25,1},{2,26},{10... | collective-permute-start | bytes 393224 | tf_op jit(solution)/shard_map/ppermute | solution.py:150
  24.1 43.7 %collective-permute-start.4 = (bf16[128,512]{1,0:T(8,128)(2,1)S(1)}, bf16[128,512]{1,0:T(8,128)(2,1)S(1)}, u32[]{:S(2)}, u32[]{:S(2)}) collective-permute-start(bf16[128,512]{1,0:T(8,128)(2,1)S(1)} %constant_dynamic-slice_fusion), channel_id=1, source_target_pairs={{0,16},{8,24},{16,0},{24,8},{1,17},{9,25},{17,1},{25,9},{2,18},{10... | collective-permute-start | bytes 393224 | tf_op jit(solution)/shard_map/ppermute | solution.py:150
  25.9 41.9 %collective-permute-start.3 = (bf16[128,512]{1,0:T(8,128)(2,1)S(1)}, bf16[128,512]{1,0:T(8,128)(2,1)S(1)}, u32[]{:S(2)}, u32[]{:S(2)}) collective-permute-start(bf16[128,512]{1,0:T(8,128)(2,1)S(1)} %constant_dynamic-slice_fusion), channel_id=1, source_target_pairs={{0,8},{8,0},{16,24},{24,16},{1,9},{9,1},{17,25},{25,17},{2,10},{10... | collective-permute-start | bytes 393224 | tf_op jit(solution)/shard_map/ppermute | solution.py:150
  33.0 34.8 %copy-start.15 = (bf16[128,512]{1,0:T(8,128)(2,1)}, bf16[128,512]{1,0:T(8,128)(2,1)S(1)}, u32[]{:S(2)}) copy-start(bf16[128,512]{1,0:T(8,128)(2,1)S(1)} %collective-permute-done.5.refs_2_) | copy-start | bytes 393220
  67.8 0.7 copy-start.16
  68.5 0.7 copy-start.17
  70.9 14.1 %copy-start.5 = (bf16[384,512]{1,0:T(8,128)(2,1)S(1)}, bf16[384,512]{1,0:T(8,128)(2,1)}, u32[]{:S(2)}) copy-start(bf16[384,512]{1,0:T(8,128)(2,1)} %shard_map.101.refs_4_) | copy-start | bytes 1179652
  70.9 22.0 %collective-permute-start.11 = (bf16[384,512]{1,0:T(8,128)(2,1)}, bf16[384,512]{1,0:T(8,128)(2,1)S(1)}, u32[]{:S(2)}, u32[]{:S(2)}) collective-permute-start(bf16[384,512]{1,0:T(8,128)(2,1)} %shard_map.101.refs_4_), channel_id=1, source_target_pairs={{0,2},{1,3},{2,0},{3,1},{4,6},{5,7},{6,4},{7,5},{8,10},{9,11},{10,... | collective-permute-start | bytes 1179656 | tf_op jit(solution)/shard_map/ppermute | solution.py:150
  72.4 12.6 %collective-permute-start.1 = (bf16[128,1024]{1,0:T(8,128)(2,1)S(1)}, bf16[128,1024]{1,0:T(8,128)(2,1)S(1)}, u32[]{:S(2)}, u32[]{:S(2)}) collective-permute-start(bf16[128,1024]{1,0:T(8,128)(2,1)S(1)} %copy-done.11), channel_id=1, source_target_pairs={{0,16},{8,24},{16,0},{24,8},{1,17},{9,25},{17,1},{25,9},{2,18},{10... | collective-permute-start | bytes 786440 | tf_op jit(solution)/shard_map/ppermute | solution.py:150
  72.6 14.6 %collective-permute-start = (bf16[128,1024]{1,0:T(8,128)(2,1)S(1)}, bf16[128,1024]{1,0:T(8,128)(2,1)S(1)}, u32[]{:S(2)}, u32[]{:S(2)}) collective-permute-start(bf16[128,1024]{1,0:T(8,128)(2,1)S(1)} %copy-done.11), channel_id=1, source_target_pairs={{0,8},{8,0},{16,24},{24,16},{1,9},{9,1},{17,25},{25,17},{2,10},{10... | collective-permute-start | bytes 786440 | tf_op jit(solution)/shard_map/ppermute | solution.py:150
  79.7 26.7 %copy-start.12 = (bf16[128,1024]{1,0:T(8,128)(2,1)}, bf16[128,1024]{1,0:T(8,128)(2,1)S(1)}, u32[]{:S(2)}) copy-start(bf16[128,1024]{1,0:T(8,128)(2,1)S(1)} %collective-permute-done.2.refs_3_) | copy-start | bytes 786436
  79.7 11.6 %collective-permute-start.14 = (bf16[528,256]{1,0:T(8,128)(2,1)}, bf16[528,256]{1,0:T(8,128)(2,1)S(1)}, u32[]{:S(2)}, u32[]{:S(2)}) collective-permute-start(bf16[528,256]{1,0:T(8,128)(2,1)} %get-tuple-element.30.refs_1_), channel_id=1, source_target_pairs={{0,8},{8,0},{16,24},{24,16},{1,9},{9,1},{17,25},{25,17},{2,10},{10... | collective-permute-start | bytes 811016 | tf_op jit(solution)/shard_map/ppermute | solution.py:150
  85.0 21.4 %copy-start.13 = (bf16[128,1024]{1,0:T(8,128)(2,1)}, bf16[128,1024]{1,0:T(8,128)(2,1)S(1)}, u32[]{:S(2)}) copy-start(bf16[128,1024]{1,0:T(8,128)(2,1)S(1)} %collective-permute-done.1.refs_2_) | copy-start | bytes 786436
  85.0 10.2 %collective-permute-start.10 = (bf16[384,512]{1,0:T(8,128)(2,1)S(1)}, bf16[384,512]{1,0:T(8,128)(2,1)S(1)}, u32[]{:S(2)}, u32[]{:S(2)}) collective-permute-start(bf16[384,512]{1,0:T(8,128)(2,1)S(1)} %copy-done.5), channel_id=1, source_target_pairs={{0,1},{1,0},{2,3},{3,2},{4,5},{5,4},{6,7},{7,6},{8,9},{9,8},{10,11... | collective-permute-start | bytes 1179656 | tf_op jit(solution)/shard_map/ppermute | solution.py:150
  87.2 5.6 %copy-start.14 = (bf16[128,1024]{1,0:T(8,128)(2,1)}, bf16[128,1024]{1,0:T(8,128)(2,1)S(1)}, u32[]{:S(2)}) copy-start(bf16[128,1024]{1,0:T(8,128)(2,1)S(1)} %collective-permute-done.refs_1_) | copy-start | bytes 786436
  87.2 10.3 %collective-permute-start.8 = (bf16[384,512]{1,0:T(8,128)(2,1)S(1)}, bf16[384,512]{1,0:T(8,128)(2,1)S(1)}, u32[]{:S(2)}, u32[]{:S(2)}) collective-permute-start(bf16[384,512]{1,0:T(8,128)(2,1)S(1)} %copy-done.5), channel_id=1, source_target_pairs={{0,6},{1,7},{2,4},{3,5},{4,2},{5,3},{6,0},{7,1},{8,14},{9,15},{10,... | collective-permute-start | bytes 1179656 | tf_op jit(solution)/shard_map/ppermute | solution.py:150
  91.4 1.6 copy-start.2
  91.4 14.5 %collective-permute-start.6 = (bf16[384,512]{1,0:T(8,128)(2,1)S(1)}, bf16[384,512]{1,0:T(8,128)(2,1)S(1)}, u32[]{:S(2)}, u32[]{:S(2)}) collective-permute-start(bf16[384,512]{1,0:T(8,128)(2,1)S(1)} %copy-done.5), channel_id=1, source_target_pairs={{0,4},{1,5},{2,6},{3,7},{4,0},{5,1},{6,2},{7,3},{8,12},{9,13},{10,... | collective-permute-start | bytes 1179656 | tf_op jit(solution)/shard_map/ppermute | solution.py:150
  92.9 13.5 %copy-start.18 = (bf16[384,512]{1,0:T(8,128)(2,1)}, bf16[384,512]{1,0:T(8,128)(2,1)S(1)}, u32[]{:S(2)}) copy-start(bf16[384,512]{1,0:T(8,128)(2,1)S(1)} %collective-permute-done.11.refs_6_) | copy-start | bytes 1179652
  92.9 13.1 %collective-permute-start.12 = (bf16[384,512]{1,0:T(8,128)(2,1)S(1)}, bf16[384,512]{1,0:T(8,128)(2,1)}, u32[]{:S(2)}, u32[]{:S(2)}) collective-permute-start(bf16[384,512]{1,0:T(8,128)(2,1)S(1)} %collective-permute-done.11.refs_6_), channel_id=1, source_target_pairs={{0,1},{1,0},{2,3},{3,2},{4,5},{5,4},{6,7},{7,6},{8,9},{9,8},{10,11... | collective-permute-start | bytes 1179656 | tf_op jit(solution)/shard_map/ppermute | solution.py:150
  95.3 10.8 %copy-start.19 = (bf16[384,512]{1,0:T(8,128)(2,1)}, bf16[384,512]{1,0:T(8,128)(2,1)S(1)}, u32[]{:S(2)}) copy-start(bf16[384,512]{1,0:T(8,128)(2,1)S(1)} %collective-permute-done.10.refs_5_) | copy-start | bytes 1179652
  95.3 40.1 %collective-permute-start.17 = (bf16[2048,256]{1,0:T(8,128)(2,1)}, bf16[2048,256]{1,0:T(8,128)(2,1)}, u32[]{:S(2)}, u32[]{:S(2)}) collective-permute-start(bf16[2048,256]{1,0:T(8,128)(2,1)} %get-tuple-element.31), channel_id=1, source_target_pairs={{0,8},{8,0},{16,24},{24,16},{1,9},{9,1},{17,25},{25,17},{2,10},{10... | collective-permute-start | bytes 3145736 | tf_op jit(solution)/shard_map/ppermute | solution.py:150
  97.6 21.5 %copy-start.6 = (bf16[384,512]{1,0:T(8,128)(2,1)}, bf16[384,512]{1,0:T(8,128)(2,1)S(1)}, u32[]{:S(2)}) copy-start(bf16[384,512]{1,0:T(8,128)(2,1)S(1)} %collective-permute-done.8.refs_6_) | copy-start | bytes 1179652
  97.6 36.3 %collective-permute-start.15 = (bf16[2080,256]{1,0:T(8,128)(2,1)}, bf16[2080,256]{1,0:T(8,128)(2,1)S(1)}, u32[]{:S(2)}, u32[]{:S(2)}) collective-permute-start(bf16[2080,256]{1,0:T(8,128)(2,1)} %shard_map.105), channel_id=1, source_target_pairs={{16,8},{8,16},{17,9},{9,17},{18,10},{10,18},{19,11},{11,19},{20,12... | collective-permute-start | bytes 3194888 | tf_op jit(solution)/shard_map/ppermute | solution.py:252
  98.3 46.1 %collective-permute-start.20 = (bf16[2080,256]{1,0:T(8,128)(2,1)}, bf16[2080,256]{1,0:T(8,128)(2,1)}, u32[]{:S(2)}, u32[]{:S(2)}) collective-permute-start(bf16[2080,256]{1,0:T(8,128)(2,1)} %collective-permute-done.19.refs_3_.refs_7_.refs_8_.refs_9_.refs_10_), channel_id=1, source_target_pairs={{8,0},{16,24},{9,1},{17,25},{10,2},{18,26},{11,3},{19,27},{12,4},{... | collective-permute-start | bytes 3194888 | tf_op jit(solution)/shard_map/ppermute | solution.py:253
  105.9 13.2 %copy-start.7 = (bf16[384,512]{1,0:T(8,128)(2,1)}, bf16[384,512]{1,0:T(8,128)(2,1)S(1)}, u32[]{:S(2)}) copy-start(bf16[384,512]{1,0:T(8,128)(2,1)S(1)} %collective-permute-done.6.refs_4_) | copy-start | bytes 1179652
  105.9 13.2 %collective-permute-start.9 = (bf16[384,512]{1,0:T(8,128)(2,1)S(1)}, bf16[384,512]{1,0:T(8,128)(2,1)S(1)}, u32[]{:S(2)}, u32[]{:S(2)}) collective-permute-start(bf16[384,512]{1,0:T(8,128)(2,1)S(1)} %collective-permute-done.8.refs_6_), channel_id=1, source_target_pairs={{0,1},{1,0},{2,3},{3,2},{4,5},{5,4},{6,7},{7,6},{8,9},{9,8},{10,11... | collective-permute-start | bytes 1179656 | tf_op jit(solution)/shard_map/ppermute | solution.py:150
  106.0 13.2 %collective-permute-start.7 = (bf16[384,512]{1,0:T(8,128)(2,1)S(1)}, bf16[384,512]{1,0:T(8,128)(2,1)S(1)}, u32[]{:S(2)}, u32[]{:S(2)}) collective-permute-start(bf16[384,512]{1,0:T(8,128)(2,1)S(1)} %collective-permute-done.6.refs_4_), channel_id=1, source_target_pairs={{0,1},{1,0},{2,3},{3,2},{4,5},{5,4},{6,7},{7,6},{8,9},{9,8},{10,11... | collective-permute-start | bytes 1179656 | tf_op jit(solution)/shard_map/ppermute | solution.py:150
  119.1 2.1 copy-start.8
  119.1 81.4 %collective-permute-start.13 = (bf16[1024,256]{1,0:T(8,128)(2,1)}, bf16[1024,256]{1,0:T(8,128)(2,1)S(1)}, u32[]{:S(2)}, u32[]{:S(2)}) collective-permute-start(bf16[1024,256]{1,0:T(8,128)(2,1)} %get-tuple-element.28), channel_id=1, source_target_pairs={{0,8},{8,0},{16,24},{24,16},{1,9},{9,1},{17,25},{25,17},{2,10},{10... | collective-permute-start | bytes 1572872 | tf_op jit(solution)/shard_map/ppermute | solution.py:150
  119.2 2.0 copy-start.9
  119.2 47.9 %collective-permute-start.24 = (bf16[1024,256]{1,0:T(8,128)(2,1)}, bf16[1024,256]{1,0:T(8,128)(2,1)S(1)}, u32[]{:S(2)}, u32[]{:S(2)}) collective-permute-start(bf16[1024,256]{1,0:T(8,128)(2,1)} %get-tuple-element.37), channel_id=1, source_target_pairs={{0,8},{8,0},{16,24},{24,16},{1,9},{9,1},{17,25},{25,17},{2,10},{10... | collective-permute-start | bytes 1572872 | tf_op jit(solution)/shard_map/ppermute | solution.py:150
  133.9 30.0 %copy-start = (bf16[2080,256]{1,0:T(8,128)(2,1)}, bf16[2080,256]{1,0:T(8,128)(2,1)S(1)}, u32[]{:S(2)}) copy-start(bf16[2080,256]{1,0:T(8,128)(2,1)S(1)} %collective-permute-done.15.refs_3_.refs_7_.refs_8_.refs_9_.refs_10_) | copy-start | bytes 3194884
  133.9 55.2 %collective-permute-start.16 = (bf16[2080,256]{1,0:T(8,128)(2,1)S(1)}, bf16[2080,256]{1,0:T(8,128)(2,1)S(1)}, u32[]{:S(2)}, u32[]{:S(2)}) collective-permute-start(bf16[2080,256]{1,0:T(8,128)(2,1)S(1)} %collective-permute-done.15.refs_3_.refs_7_.refs_8_.refs_9_.refs_10_), channel_id=1, source_target_pairs={{8,0},{16,24},{9,1},{17,25},{10,2},{18,26},{11,3},{19,27},{12,4},{... | collective-permute-start | bytes 3194888 | tf_op jit(solution)/shard_map/ppermute | solution.py:253
  164.9 35.0 %collective-permute-start.23 = (f32[4]{0:T(128)S(1)}, f32[4]{0:T(128)S(1)}, u32[]{:S(2)}, u32[]{:S(2)}) collective-permute-start(f32[4]{0:T(128)S(1)} %reduce_sum.9), channel_id=1, source_target_pairs={{0,24},{8,16},{16,8},{24,0},{1,25},{9,17},{17,9},{25,1},{2,26},{10... | collective-permute-start | bytes 56 | tf_op jit(solution)/shard_map/ppermute | solution.py:150
  167.2 32.7 %collective-permute-start.22 = (f32[4]{0:T(128)S(1)}, f32[4]{0:T(128)S(1)}, u32[]{:S(2)}, u32[]{:S(2)}) collective-permute-start(f32[4]{0:T(128)S(1)} %reduce_sum.9), channel_id=1, source_target_pairs={{0,16},{8,24},{16,0},{24,8},{1,17},{9,25},{17,1},{25,9},{2,18},{10... | collective-permute-start | bytes 56 | tf_op jit(solution)/shard_map/ppermute | solution.py:150
  167.2 22.0 %copy-start.4 = (bf16[1024,256]{1,0:T(8,128)(2,1)}, bf16[1024,256]{1,0:T(8,128)(2,1)S(1)}, u32[]{:S(2)}) copy-start(bf16[1024,256]{1,0:T(8,128)(2,1)S(1)} %collective-permute-done.24.refs_2_) | copy-start | bytes 1572868
  167.2 32.7 %collective-permute-start.21 = (f32[4]{0:T(128)S(1)}, f32[4]{0:T(128)S(1)}, u32[]{:S(2)}, u32[]{:S(2)}) collective-permute-start(f32[4]{0:T(128)S(1)} %reduce_sum.9), channel_id=1, source_target_pairs={{0,8},{8,0},{16,24},{24,16},{1,9},{9,1},{17,25},{25,17},{2,10},{10... | collective-permute-start | bytes 56 | tf_op jit(solution)/shard_map/ppermute | solution.py:150
  189.1 1.0 copy-start.1
  200.5 0.8 copy-start.3
